TPU v7x, 128 devices: a whole 4x4x4 slice. The times are simulated.
128 devices in a mesh: data: 128 (over z, y, x, core).
Axes of the slice: x: 4, y: 4, z: 4, core: 2. Of those that a mesh axis runs over, the one named last changes fastest.
Arguments:
- act_in: bfloat16 [131072, 768], P('data')
- grad_out: bfloat16 [131072, 768], P('data')
- w_up: bfloat16 [2, 768, 3072], replicated
- w_down: bfloat16 [2, 3072, 768], replicated
- master_up: float32 [2, 768, 3072], P(None, 'data')
- master_down: float32 [2, 3072, 768], P(None, 'data')
- exp_avg_up: float32 [2, 768, 3072], P(None, 'data')
- exp_avg_down: float32 [2, 3072, 768], P(None, 'data')
- exp_sq_up: float32 [2, 768, 3072], P(None, 'data')
- exp_sq_down: float32 [2, 3072, 768], P(None, 'data')
- learn_rate: float32 [], replicated
- clip_norm: float32 [], replicated
Outputs:
- output 1: bfloat16 [2, 768, 3072], replicated
- output 2: bfloat16 [2, 3072, 768], replicated
- output 3: float32 [2, 768, 3072], P(None, 'data')
- output 4: float32 [2, 3072, 768], P(None, 'data')
- output 5: float32 [2, 768, 3072], P(None, 'data')
- output 6: float32 [2, 3072, 768], P(None, 'data')
- output 7: float32 [2, 768, 3072], P(None, 'data')
- output 8: float32 [2, 3072, 768], P(None, 'data')
- output 9: float32 [], replicated
All inputs are finite; a program needn't handle non-finite values.
Results may differ from a plain program's by a relative error of at most 0.00398.
Values are sent between devices in bfloat16 or wider.
A program may use at most 1 GiB of HBM per device.

v0:
```python
import functools
import math

import jax
import jax.numpy as jnp
from jax import lax
from jax.experimental import pallas as pl
from jax.experimental.pallas import tpu as pltpu
from jax.sharding import PartitionSpec as P

STEP = 10
BETA_ONE = 0.9
BETA_TWO = 0.95
ADAM_EPS = 1e-8
NORM_EPS = 1e-6
INV_SQRT_TWO = 0.7071067811865476
INV_SQRT_TWO_PI = 0.3989422804014327

MESH = pl.DeviceIdType.MESH
RING = 4
ROWS = 48
HALF = 24
LANES = 128
F32 = jnp.float32
BF16 = jnp.bfloat16


def gelu_parts(pre_act):
    normal_cdf = 0.5 * (1.0 + lax.erf(pre_act * INV_SQRT_TWO))
    normal_pdf = jnp.exp(-0.5 * pre_act * pre_act) * INV_SQRT_TWO_PI
    return pre_act * normal_cdf, normal_cdf + pre_act * normal_pdf


def local_grads(act_in, grad_out, w_up, w_down):
    z_one = jnp.einsum("td,df->tf", act_in, w_up[0], preferred_element_type=jnp.float32)
    gelu_one, slope_one = gelu_parts(z_one)
    act_one = gelu_one.astype(jnp.bfloat16)
    hidden = jnp.einsum("tf,fd->td", act_one, w_down[0], preferred_element_type=jnp.float32).astype(jnp.bfloat16)
    z_three = jnp.einsum("td,df->tf", hidden, w_up[1], preferred_element_type=jnp.float32)
    gelu_three, slope_three = gelu_parts(z_three)
    act_three = gelu_three.astype(jnp.bfloat16)
    g_four = jnp.einsum("tf,td->fd", act_three, grad_out, preferred_element_type=jnp.float32)
    dz_three = (jnp.einsum("td,fd->tf", grad_out, w_down[1], preferred_element_type=jnp.float32) * slope_three).astype(jnp.bfloat16)
    g_three = jnp.einsum("td,tf->df", hidden, dz_three, preferred_element_type=jnp.float32)
    d_hidden = jnp.einsum("tf,df->td", dz_three, w_up[1], preferred_element_type=jnp.float32).astype(jnp.bfloat16)
    g_two = jnp.einsum("tf,td->fd", act_one, d_hidden, preferred_element_type=jnp.float32)
    dz_one = (jnp.einsum("td,fd->tf", d_hidden, w_down[0], preferred_element_type=jnp.float32) * slope_one).astype(jnp.bfloat16)
    g_one = jnp.einsum("td,tf->df", act_in, dz_one, preferred_element_type=jnp.float32)
    return g_one, g_two, g_three, g_four


def adam_direction(exp_avg, exp_sq, grad, clip_scale):
    bias_one = 1.0 - BETA_ONE ** STEP
    bias_two = 1.0 - BETA_TWO ** STEP
    avg_new = BETA_ONE * exp_avg + (1.0 - BETA_ONE) * clip_scale * grad
    sq_new = BETA_TWO * exp_sq + (1.0 - BETA_TWO) * (clip_scale * clip_scale) * (grad * grad)
    direction = (avg_new / bias_one) / (jnp.sqrt(sq_new / bias_two) + ADAM_EPS)
    return avg_new, sq_new, direction


class Unit:
    def __init__(self, kind, k, off, cols, order):
        self.kind, self.k, self.off, self.cols, self.order = kind, k, off, cols, order
        self.dims = "zy" if kind == "up" else "zyx"
        self.shape = (RING,) * len(self.dims) + (ROWS, cols)

    def half(self, phase, dest, h, me):
        if self.kind == "up" and phase == 2:
            return (dest, h), (6, self.cols)
        fixed = {d: me[d] for d in self.order[:phase]}
        fixed[self.order[phase]] = dest
        index, shape, split = [], [], False
        for d in self.dims:
            if d in fixed:
                index.append(fixed[d])
            elif not split:
                index.append(pl.ds(2 * h, 2))
                shape.append(2)
                split = True
            else:
                index.append(slice(None))
                shape.append(RING)
        if split:
            return tuple(index), tuple(shape) + (ROWS, self.cols)
        return tuple(index) + (pl.ds(HALF * h, HALF),), (HALF, self.cols)

    def half_shape(self, phase):
        return self.half(phase, 0, 0, dict(x=0, y=0, z=0))[1]


def make_units(up_cols, down_cols):
    u, d = up_cols // 2, down_cols // 3
    return [
        Unit("down", 1, 0, 2 * d, "xyz"),
        Unit("up", 1, 0, u, "zyx"),
        Unit("up", 1, u, u, "yzx"),
        Unit("down", 1, 2 * d, d, "yxz"),
        Unit("down", 0, 0, 2 * d, "xzy"),
        Unit("down", 0, 2 * d, d, "zxy"),
        Unit("up", 0, 0, u, "zyx"),
        Unit("up", 0, u, u, "yzx"),
    ]


def serve_order(ready, phases, tail):
    rate, hop, work = 46600.0, 2.5, 0.4
    link, now, events = {}, 0.0, []
    ready, state, late = list(ready), [0] * len(ready), [0.0] * len(ready)
    ends = [2 * len(p) + tail for p in phases]

    def send(phase):
        d, nbytes = phase
        for sign in "+-":
            link[d, sign] = max(link.get((d, sign), 0.0), now) + nbytes / rate
        return max(link[d, sign] for sign in "+-") + hop

    while any(s <= e for s, e in zip(state, ends)):
        i = min((j for j in range(len(ready)) if state[j] <= ends[j]), key=lambda j: (ready[j], j))
        phase, middle = divmod(state[i], 2)
        events.append((i, state[i]))
        now = max(now, ready[i]) + work
        if phase < len(phases[i]):
            ready[i] = send(phases[i][phase])
            if middle:
                ready[i] = max(ready[i], late[i])
            else:
                late[i] = send(phases[i][phase])
        else:
            ready[i] = now + hop
        state[i] += 1
    return events


def half_bytes(shape, dtype):
    return math.prod(shape) * jnp.dtype(dtype).itemsize


def position():
    me = lax.axis_index("data")
    return dict(z=me // 32, y=(me // 8) % RING, x=(me // 2) % RING, c=me % 2)


def device_of(at):
    return (((at["z"] * RING + at["y"]) * RING + at["x"]) * 2 + at["c"],)


def moved(me, d, by):
    return device_of({**me, d: (me[d] + by) % RING})


def partner_of(me):
    return device_of({**me, "c": 1 - me["c"]})


def group_peers(me):
    first, second = [], []
    j, q = me["x"] * 2 + me["c"], me["z"] * 4 + me["y"]
    for t in range(1, 8):
        o = (j + t) % 8
        first.append((o, device_of({**me, "x": o // 2, "c": o % 2})))
    for t in range(1, 16):
        o = (q + t) % 16
        second.append((o, device_of({**me, "z": o // 4, "y": o % RING})))
    return first, second


def remote(src, dst, send_sem, recv_sem, device):
    return pltpu.make_async_remote_copy(src_ref=src, dst_ref=dst, send_sem=send_sem, recv_sem=recv_sem, device_id=device, device_id_type=MESH)


def add_into(dst, *srcs):
    lead = dst.shape[:-2]
    if not lead:
        dst[...] = functools.reduce(lambda a, b: a + b, [s[...] for s in srcs], dst[...])
        return

    def body(i, carry):
        index = []
        for n in reversed(lead):
            index.append(i % n)
            i = i // n
        index = tuple(reversed(index))
        dst[index] = functools.reduce(lambda a, b: a + b, [s[index] for s in srcs], dst[index])
        return carry

    lax.fori_loop(0, math.prod(lead), body, 0)


def reduce_update_kernel(units, events, *refs):
    n_units = len(units)
    take = iter(refs)
    g_ref = {("up", 0): next(take), ("down", 0): next(take), ("up", 1): next(take), ("down", 1): next(take)}
    master = dict(up=next(take), down=next(take))
    avg = dict(up=next(take), down=next(take))
    sq = dict(up=next(take), down=next(take))
    rate_ref, clip_ref = next(take), next(take)
    weight = dict(up=next(take), down=next(take))
    master_out = dict(up=next(take), down=next(take))
    avg_out = dict(up=next(take), down=next(take))
    sq_out = dict(up=next(take), down=next(take))
    norm_ref = next(take)
    acc = [next(take) for _ in units]
    recv = [[[next(take) for _ in range(6)] for _ in range(3)] for _ in units]
    xbuf = {i: next(take) for i, u in enumerate(units) if u.kind == "up"}
    fin = [next(take) for _ in units]
    slots = {}
    slot_of = {}
    for i, u in enumerate(units):
        if (u.kind, u.cols, u.off) not in slots:
            slots[u.kind, u.cols, u.off] = next(take)
        slot_of[i] = slots[u.kind, u.cols, u.off]
    grad = dict(up=next(take), down=next(take))
    small_src, small_one, small_two = next(take), next(take), next(take)
    load_sem, pair_send, pair_recv, ring_send, ring_recv, fin_send, fin_recv = [next(take) for _ in range(7)]
    one_send, one_recv, two_send, two_recv = [next(take) for _ in range(4)]

    me = position()
    core = me["c"]
    partner = partner_of(me)
    first, second = group_peers(me)

    barrier = pltpu.get_barrier_semaphore()
    for _, device in first + second:
        pl.semaphore_signal(barrier, inc=1, device_id=device, device_id_type=MESH)
    pl.semaphore_wait(barrier, len(first) + len(second))

    def columns(u, c):
        ref = g_ref[u.kind, u.k]
        width = ref.shape[-1] // 2
        start = pl.multiple_of(c * width + u.off, LANES)
        return ref.at[(slice(None),) * (len(ref.shape) - 1) + (pl.ds(start, u.cols),)]

    pair_copy = [remote(columns(u, 1 - core), acc[i], pair_send.at[i], pair_recv.at[i], partner) for i, u in enumerate(units)]
    load_copy = [pltpu.make_async_copy(columns(u, core), slot_of[i], load_sem.at[i]) for i, u in enumerate(units)]
    later = {}
    for i, u in enumerate(units):
        earlier = [j for j in range(i) if slot_of[j] is slot_of[i]]
        if earlier:
            later[earlier[-1]] = i
        else:
            load_copy[i].start()
        pair_copy[i].start()

    sent = []

    def ring(i, phase, n):
        u = units[i]
        d = u.order[phase]
        base = xbuf[i] if u.kind == "up" and phase == 2 else acc[i]
        by = 1 if n % 2 == 0 else -1
        dest = (me[d] + (2 if n < 2 else by)) % RING
        h = (0, 1, 1, 0, 0, 1)[n]
        src = base.at[u.half(phase, dest, h, me)[0]]
        s = (i * 3 + phase) * 6 + n
        return remote(src, recv[i][phase][n], ring_send.at[s], ring_recv.at[s], moved(me, d, by)), src

    def start_phase(i, phase):
        u = units[i]
        if u.kind == "up" and phase == 2:
            block = acc[i][me["z"], me["y"]]
            for p in range(8):
                xbuf[i][p // 2, p % 2] = block[6 * p:6 * p + 6]
        for n in range(4):
            copy, _ = ring(i, phase, n)
            copy.start()
            sent.append(copy)

    for i, s in events:
        u = units[i]
        if s == 0:
            load_copy[i].wait()
            pair_copy[i].wait_recv()
            add_into(acc[i], slot_of[i])
            if i in later:
                load_copy[later[i]].start()
            start_phase(i, 0)
        elif s < 7 and s % 2 == 1:
            phase = (s - 1) // 2
            for n in (4, 5):
                copy, src = ring(i, phase, n)
                ring(i, phase, n - 4)[0].wait_recv()
                add_into(src, recv[i][phase][n - 4])
                copy.start()
                sent.append(copy)
        elif s < 7:
            phase = s // 2 - 1
            d = u.order[phase]
            base = xbuf[i] if u.kind == "up" and phase == 2 else acc[i]
            for n in (2, 3, 4, 5):
                ring(i, phase, n)[0].wait_recv()
            for h, (a, b) in enumerate(((4, 3), (2, 5))):
                add_into(base.at[u.half(phase, me[d], h, me)[0]], recv[i][phase][a], recv[i][phase][b])
            if phase < 2:
                start_phase(i, phase + 1)
            else:
                src = xbuf[i].at[me["x"], 1 - core] if u.kind == "up" else acc[i].at[me["z"], me["y"], me["x"], pl.ds(pl.multiple_of(HALF * (1 - core), 8), HALF)]
                copy = remote(src, fin[i], fin_send.at[i], fin_recv.at[i], partner)
                copy.start()
                sent.append(copy)
        else:
            src = xbuf[i].at[me["x"], core] if u.kind == "up" else acc[i].at[me["z"], me["y"], me["x"], pl.ds(pl.multiple_of(HALF * core, 8), HALF)]
            remote(src, fin[i], fin_send.at[i], fin_recv.at[i], partner).wait_recv()
            own, other = src[...], fin[i][...]
            half = grad[u.kind].shape[-1] // 2
            grad[u.kind][u.k, :, u.off:u.off + u.cols] = jnp.where(core == 0, own, other) * (1.0 / 128.0)
            grad[u.kind][u.k, :, half + u.off:half + u.off + u.cols] = jnp.where(core == 0, other, own) * (1.0 / 128.0)

    def total(values):
        row = lax.broadcasted_iota(jnp.int32, (8, LANES), 0)
        tile = jnp.zeros((8, LANES), F32)
        for r, value in enumerate(values):
            tile = jnp.where(row == r, value, tile)
        return tile

    def all_sum(at, tile):
        for stage, (peers, own, buf, send, recv_s) in enumerate((
            (first, me["x"] * 2 + core, small_one, one_send, one_recv),
            (second, me["z"] * 4 + me["y"], small_two, two_send, two_recv),
        )):
            small_src[at, stage] = tile
            buf[at, own] = tile
            for t, (o, device) in enumerate(peers):
                copy = remote(small_src.at[at, stage], buf.at[at, own], send.at[at, t], recv_s.at[at, own], device)
                copy.start()
                sent.append(copy)
            for o, device in peers:
                remote(small_src.at[at, stage], buf.at[at, o], send.at[at, 0], recv_s.at[at, o], device).wait_recv()
            tile = buf[at, 0]
            for o in range(1, len(peers) + 1):
                tile = tile + buf[at, o]
        return tile

    def squares(x):
        return jnp.sum(x * x)

    def rows(kind, k):
        return (slice(None), k) if kind == "up" else (k,)

    keys = (("up", 0), ("down", 0), ("up", 1), ("down", 1))
    local_sq = functools.reduce(lambda a, b: a + b, [squares(grad[kind][k]) for kind, k in keys])
    sums = all_sum(0, total([local_sq] + [squares(master[kind][rows(kind, k)]) for kind, k in keys]))
    norm = jnp.sqrt(sums[0:1, :])
    norm_ref[...] = jnp.broadcast_to(norm, norm_ref.shape)
    clip_scale = jnp.minimum(1.0, clip_ref[0] / (norm + NORM_EPS))[:, 0:1]
    master_norm = jnp.sqrt(sums)
    local = []
    for kind, k in keys:
        avg_new, sq_new, direction = adam_direction(avg[kind][rows(kind, k)], sq[kind][rows(kind, k)], grad[kind][k], clip_scale)
        avg_out[kind][rows(kind, k)] = avg_new
        sq_out[kind][rows(kind, k)] = sq_new
        grad[kind][k] = direction
        local.append(squares(direction))
    dir_norm = jnp.sqrt(all_sum(1, total(local)))
    for r, (kind, k) in enumerate(keys):
        ratio = (master_norm[r + 1:r + 2, :] / dir_norm[r:r + 1, :])[:, 0:1]
        new = master[kind][rows(kind, k)] - rate_ref[0] * ratio * grad[kind][k]
        master_out[kind][rows(kind, k)] = new
        weight[kind][k] = new.astype(BF16)

    for copy in pair_copy + sent:
        copy.wait_send()


def reduce_update(grads, master, avg, sq, learn_rate, clip_norm):
    up_cols, down_cols = grads[0].shape[1], grads[1].shape[1]
    units = make_units(up_cols // 2, down_cols // 2)
    arrive, ready = 2.0, []
    for u in units:
        arrive += half_bytes(u.shape, F32) / 550000.0
        ready.append(arrive)
    events = serve_order(ready, [[(u.order[p], half_bytes(u.half_shape(p), F32)) for p in range(3)] for u in units], 1)
    views = [g.reshape((RING, RING, ROWS, up_cols)) if i % 2 == 0 else g.reshape((RING, RING, RING, ROWS, down_cols)) for i, g in enumerate(grads)]
    scratch = [pltpu.VMEM(u.shape, F32) for u in units]
    scratch += [pltpu.VMEM(u.half_shape(p), F32) for u in units for p in range(3) for _ in range(6)]
    scratch += [pltpu.VMEM((4, 2, 6, u.cols), F32) for u in units if u.kind == "up"]
    scratch += [pltpu.VMEM((6 if u.kind == "up" else HALF, u.cols), F32) for u in units]
    seen = set()
    for u in units:
        if (u.kind, u.cols, u.off) not in seen:
            seen.add((u.kind, u.cols, u.off))
            scratch.append(pltpu.VMEM(u.shape, F32))
    master, avg, sq = [(up.transpose(1, 0, 2), down) for up, down in (master, avg, sq)]
    blocks = [(2, 6, up_cols), (2, HALF, down_cols)]
    scratch += [pltpu.VMEM(b, F32) for b in blocks]
    scratch += [pltpu.VMEM((2, 2, 8, LANES), F32), pltpu.VMEM((2, 8, 8, LANES), F32), pltpu.VMEM((2, 16, 8, LANES), F32)]
    n = len(units)
    dma = pltpu.SemaphoreType.DMA
    scratch += [dma((n,)), dma((n,)), dma((n,)), dma((n * 18,)), dma((n * 18,)), dma((n,)), dma((n,))]
    scratch += [dma((2, 7)), dma((2, 8)), dma((2, 15)), dma((2, 16))]
    vmem, smem = pl.BlockSpec(memory_space=pltpu.VMEM), pl.BlockSpec(memory_space=pltpu.SMEM)
    state = [jax.ShapeDtypeStruct(a.shape, F32) for a in master]
    outs = pl.pallas_call(
        functools.partial(reduce_update_kernel, units, events),
        out_shape=[jax.ShapeDtypeStruct(b, BF16) for b in blocks] + state * 3 + [jax.ShapeDtypeStruct((8, LANES), F32)],
        in_specs=[pl.BlockSpec(memory_space=pl.ANY)] * 4 + [vmem] * 6 + [smem] * 2,
        out_specs=[vmem] * 9,
        scratch_shapes=scratch,
        compiler_params=pltpu.CompilerParams(collective_id=0, has_side_effects=True, vmem_limit_bytes=60 * 1024 * 1024),
        name="reduce_update",
    )(*views, *master, *avg, *sq, learn_rate.reshape(1), clip_norm.reshape(1))
    return outs


class Gather:
    def __init__(self, kind, k, off, cols, order):
        self.kind, self.k, self.off, self.cols, self.order = kind, k, off, cols, order
        self.dims = "zy" if kind == "up" else "zyx"
        self.shape = (RING,) * len(self.dims) + (ROWS, cols)

    def chunk(self, phase, owner, me, h=None):
        gathered, d = self.order[:phase], self.order[phase]
        index, shape, split = [], [], h is None
        for e in self.dims:
            if e == d:
                index.append(owner)
            elif e not in gathered:
                index.append(me[e])
            elif split:
                index.append(slice(None))
                shape.append(RING)
            else:
                index.append(pl.ds(2 * h, 2))
                shape.append(2)
                split = True
        if split:
            return tuple(index), tuple(shape) + (ROWS, self.cols)
        return tuple(index) + (pl.ds(HALF * h, HALF),), (HALF, self.cols)


def make_gathers(up_cols, down_cols):
    u, d = up_cols // 2, down_cols // 3
    return [
        Gather("down", 1, 0, 2 * d, "zyx"),
        Gather("down", 0, 0, 2 * d, "yzx"),
        Gather("down", 1, 2 * d, d, "xzy"),
        Gather("down", 0, 2 * d, d, "xyz"),
        Gather("up", 1, 0, u, "yz"),
        Gather("up", 1, u, u, "zy"),
        Gather("up", 0, 0, u, "yz"),
        Gather("up", 0, u, u, "zy"),
    ]


def gather_kernel(units, events, up_ref, down_ref, out_up, out_down, *refs):
    take = iter(refs)
    block = [next(take) for _ in units]
    rows_up, rows_down, assembly = next(take), next(take), next(take)
    row_send, row_recv, core_send, core_recv, ring_send, ring_recv, own_sem, share_send, share_recv = [next(take) for _ in range(9)]
    me = position()
    core = me["c"]
    partner = partner_of(me)
    own = me["x"] * 2 + core
    first = group_peers(me)[0]
    around = [moved(me, d, by) for d in "zy" for by in (1, -1)]
    half_up, half_down = up_ref.shape[-1] // 2, down_ref.shape[-1] // 2

    barrier = pltpu.get_barrier_semaphore()
    for device in [device for _, device in first] + around:
        pl.semaphore_signal(barrier, inc=1, device_id=device, device_id_type=MESH)
    pl.semaphore_wait(barrier, len(first) + len(around))

    sent = []

    def send(copy):
        copy.start()
        sent.append(copy)

    other = pl.ds(pl.multiple_of((1 - core) * half_down, LANES), half_down)
    core_copy = remote(down_ref.at[:, :, other], rows_down, core_send, core_recv, partner)
    send(core_copy)
    for t, (o, device) in enumerate(first):
        width = pl.ds(pl.multiple_of((o % 2) * half_up, LANES), half_up)
        send(remote(up_ref.at[:, :, width], rows_up.at[own], row_send.at[t], row_recv.at[own], device))

    def part(i, phase, owner, h=None, of=core):
        u = units[i]
        out, half = (out_up, half_up) if u.kind == "up" else (out_down, half_down)
        at = u.chunk(phase, owner, me, h)[0]
        at = at + (slice(None),) * (len(u.dims) + 1 - len(at))
        return out.at[(u.k,) + at + (pl.ds(pl.multiple_of(of * half + u.off, LANES), u.cols),)]

    def ring(i, phase, n):
        d = units[i].order[phase]
        by = 1 if n % 2 == 0 else -1
        owner = me[d] if n < 4 else (me[d] - by) % RING
        ref = part(i, phase, owner, (0, 1, 1, 0, 0, 1)[n])
        s = (i * 3 + phase) * 6 + n
        return remote(ref, ref, ring_send.at[s], ring_recv.at[s], moved(me, d, by))

    def start_phase(i, phase):
        for n in range(4):
            send(ring(i, phase, n))

    shares = []

    def share(i, j, owner):
        phase = len(units[i].order) - 1
        mine, theirs = part(i, phase, owner), part(i, phase, owner, None, 1 - core)
        send(remote(mine, mine, share_send.at[i, j], share_recv.at[i, j], partner))
        shares.append(remote(theirs, theirs, share_send.at[i, j], share_recv.at[i, j], partner))

    rows_ready = [False]
    for i, s in events:
        u = units[i]
        last = len(u.order) - 1
        if s == 0:
            if u.kind == "down":
                if i == 0:
                    core_copy.wait_recv()
                low, high = down_ref[u.k, :, u.off:u.off + u.cols], down_ref[u.k, :, half_down + u.off:half_down + u.off + u.cols]
                mine = jnp.where(core == 0, low, high)
                theirs = rows_down[u.k, :, u.off:u.off + u.cols]
                block[i][...] = jnp.concatenate([jnp.where(core == 0, mine, theirs), jnp.where(core == 0, theirs, mine)], axis=0)
            else:
                if not rows_ready[0]:
                    rows_ready[0] = True
                    rows_up[own] = jnp.where(core == 0, up_ref[:, :, :half_up], up_ref[:, :, half_up:])
                    for o, device in first:
                        remote(rows_up.at[o], rows_up.at[o], row_send.at[0], row_recv.at[o], device).wait_recv()
                for p in range(8):
                    assembly[6 * p:6 * p + 6, :] = rows_up[p, u.k, :, u.off:u.off + u.cols].astype(F32)
                block[i][...] = assembly[...].astype(BF16)
            own_copy = pltpu.make_async_copy(block[i], part(i, 0, me[u.order[0]]), own_sem.at[i])
            own_copy.start()
            own_copy.wait()
            start_phase(i, 0)
        elif s % 2 == 1:
            phase = (s - 1) // 2
            if phase == last:
                share(i, 0, me[u.order[last]])
            for n in (4, 5):
                d = u.order[phase]
                incoming = part(i, phase, (me[d] + (-1 if n == 4 else 1)) % RING, n - 4)
                remote(incoming, incoming, ring_send.at[0], ring_recv.at[(i * 3 + phase) * 6 + n - 4], moved(me, d, 1)).wait_recv()
                send(ring(i, phase, n))
        else:
            phase = s // 2 - 1
            d = u.order[phase]
            for n in (2, 3, 4, 5):
                step = {2: -1, 3: 1, 4: -2, 5: 2}[n]
                h = {2: 1, 3: 0, 4: 0, 5: 1}[n]
                incoming = part(i, phase, (me[d] + step) % RING, h)
                remote(incoming, incoming, ring_send.at[0], ring_recv.at[(i * 3 + phase) * 6 + n], moved(me, d, 1)).wait_recv()
                if phase == last and n == 3:
                    share(i, 1, (me[d] - 1) % RING)
                    share(i, 2, (me[d] + 1) % RING)
            if phase < last:
                start_phase(i, phase + 1)
            else:
                share(i, 3, (me[d] + 2) % RING)

    for copy in shares:
        copy.wait_recv()
    for copy in sent:
        copy.wait_send()


def gather_weights(block_up, block_down):
    up_cols, down_cols = block_up.shape[2], block_down.shape[2]
    units = make_gathers(up_cols // 2, down_cols // 2)
    here = dict(x=0, y=0, z=0)
    events = serve_order([2.0 if u.kind == "down" else 6.0 for u in units], [[(d, half_bytes(u.chunk(p, 0, here, 0)[1], BF16)) for p, d in enumerate(u.order)] for u in units], 0)
    n = len(units)
    dma = pltpu.SemaphoreType.DMA
    scratch = [pltpu.VMEM((ROWS, u.cols), BF16) for u in units]
    scratch += [pltpu.VMEM((8, 2, 6, up_cols // 2), BF16), pltpu.VMEM((2, HALF, down_cols // 2), BF16), pltpu.VMEM((ROWS, up_cols // 4), F32)]
    scratch += [dma((7,)), dma((8,)), dma, dma, dma((n * 18,)), dma((n * 18,)), dma((n,)), dma((n, 4)), dma((n, 4))]
    vmem = pl.BlockSpec(memory_space=pltpu.VMEM)
    out_up, out_down = pl.pallas_call(
        functools.partial(gather_kernel, units, events),
        out_shape=[jax.ShapeDtypeStruct((2, RING, RING, ROWS, up_cols), BF16), jax.ShapeDtypeStruct((2, RING, RING, RING, ROWS, down_cols), BF16)],
        in_specs=[vmem] * 2,
        out_specs=[pl.BlockSpec(memory_space=pl.ANY)] * 2,
        scratch_shapes=scratch,
        compiler_params=pltpu.CompilerParams(collective_id=1, has_side_effects=True, vmem_limit_bytes=HALF * 1024 * 1024),
        name="gather_weights",
    )(block_up, block_down)
    return out_up, out_down


def finish_kernel(*refs):
    n = (len(refs) - 1) // 2
    copies = []
    for i in range(n):
        src, dst = refs[i], refs[n + i]
        for j in range(src.shape[0] * 2 if len(src.shape) > 3 else 1):
            at = (j // 2, pl.ds(j % 2 * 2, 2)) if len(src.shape) > 3 else slice(None)
            copies.append(pltpu.make_async_copy(src.at[at], dst.at[at], refs[-1].at[i, j]))
    for copy in copies:
        copy.start()
    for copy in copies:
        copy.wait()


def finish(arrays):
    any_space = pl.BlockSpec(memory_space=pl.ANY)
    return pl.pallas_call(
        finish_kernel,
        out_shape=[jax.ShapeDtypeStruct(a.shape, a.dtype) for a in arrays],
        in_specs=[any_space] * len(arrays),
        out_specs=[any_space] * len(arrays),
        scratch_shapes=[pltpu.SemaphoreType.DMA((len(arrays), 4))],
        compiler_params=pltpu.CompilerParams(vmem_limit_bytes=1024 * 1024),
        name="finish",
    )(*arrays)


def solution(mesh):
    batch_rows = P("data", None)
    state_rows = P(None, "data", None)
    replicated = P()

    def device_step(act_in, grad_out, w_up, w_down, master_up, master_down, exp_avg_up, exp_avg_down, exp_sq_up, exp_sq_down, learn_rate, clip_norm):
        grads = local_grads(act_in, grad_out, w_up, w_down)
        outs = reduce_update(grads, (master_up, master_down), (exp_avg_up, exp_avg_down), (exp_sq_up, exp_sq_down), learn_rate, clip_norm)
        new_w_up, new_w_down, *state, norm = finish((*gather_weights(*outs[:2]), *outs[2:]))
        state = [a.transpose(1, 0, 2) if i % 2 == 0 else a for i, a in enumerate(state)]
        return (new_w_up.reshape(w_up.shape), new_w_down.reshape(w_down.shape), *state, norm[0, 0])

    return jax.shard_map(device_step, mesh=mesh, in_specs=(batch_rows, batch_rows, replicated, replicated, state_rows, state_rows, state_rows, state_rows, state_rows, state_rows, replicated, replicated), out_specs=(replicated, replicated, state_rows, state_rows, state_rows, state_rows, state_rows, state_rows, replicated), check_vma=False)
```

profile of v0, /device:TPU:1, one launch (start us, length us, event | category | flops | bytes accessed | tf_op | source)
XLA Modules:
  0.0 292.8 jit_solution(9880861993714907442)
XLA Ops:
  0.6 0.0 copy-start
  2.1 0.0 copy-done
  2.1 0.0 copy-start.11
  2.1 0.0 slice-start
  2.1 0.0 slice-start.1
  2.1 12.8 %multiply_convert_fusion.1 = (bf16[1024,3072]{1,0:T(8,128)(2,1)S(1)}, f32[1024,3072]{1,0:T(8,128)}) fusion(bf16[1024,768]{1,0:T(8,128)(2,1)S(1)} %copy-done, bf16[2,768,3072]{2,1,0:T(8,128)(2,1)} %param.14), kind=kOutput, calls=%fused_computation.16 | convolution fusion | flops 4847566848 | bytes 25165824 | tf_op jit(solution)/shard_map/td,df->tf/dot_general | solution.py:35
  14.9 2.6 copy-done.17
  17.5 0.0 copy-done.11
  17.5 5.1 %fusion.29 = bf16[1024,768]{1,0:T(8,128)(2,1)S(1)} fusion(bf16[1024,3072]{1,0:T(8,128)(2,1)S(1)} %get-tuple-element.49, bf16[2,3072,768]{2,1,0:T(8,128)(2,1)S(1)} %copy-done.11), kind=kOutput, calls=%fused_computation.35 | convolution fusion | flops 4832624640 | bytes 12582912 | tf_op jit(solution)/shard_map/tf,fd->td/dot_general | solution.py:38
  22.6 1.1 copy-done.15
  23.7 0.0 copy-start.12
  23.7 7.9 %fusion.15 = f32[1024,3072]{1,0:T(8,128)} fusion(bf16[1024,768]{1,0:T(8,128)(2,1)S(1)} %fusion.29, bf16[2,768,3072]{2,1,0:T(8,128)(2,1)S(1)} %bitcast.63), kind=kOutput, calls=%fused_computation.21 | convolution fusion | flops 4831838208 | bytes 18874368 | tf_op jit(solution)/shard_map/td,df->tf/dot_general | solution.py:39
  31.7 12.2 %fusion.5 = bf16[1024,3072]{1,0:T(8,128)(2,1)S(1)} fusion(f32[1024,3072]{1,0:T(8,128)} %fusion.15, bf16[1024,768]{1,0:T(8,128)(2,1)S(1)} %copy-done.12, bf16[2,3072,768]{2,1,0:T(8,128)(2,1)S(1)} %copy-done.11), kind=kOutput, calls=%fused_computation.7 | convolution fusion | flops 4863295488 | bytes 25165824 | tf_op jit(solution)/shard_map/td,fd->tf/dot_general | solution.py:43
  43.9 13.4 %fusion.12 = f32[3072,768]{1,0:T(8,128)} fusion(bf16[1024,768]{1,0:T(8,128)(2,1)S(1)} %copy-done.12, f32[1024,3072]{1,0:T(8,128)} %fusion.15), kind=kOutput, calls=%fused_computation.18 | convolution fusion | flops 4847566848 | bytes 23592960 | tf_op jit(solution)/shard_map/tf,td->fd/dot_general | solution.py:42
  57.3 5.1 %fusion.32 = bf16[1024,768]{1,0:T(8,128)(2,1)S(1)} fusion(bf16[1024,3072]{1,0:T(8,128)(2,1)S(1)} %fusion.5, bf16[2,768,3072]{2,1,0:T(8,128)(2,1)S(1)} %bitcast.63), kind=kOutput, calls=%fused_computation.36 | convolution fusion | flops 4832624640 | bytes 12582912 | tf_op jit(solution)/shard_map/tf,df->td/dot_general | solution.py:45
  62.3 16.5 %fusion.36 = f32[3072,768]{0,1:T(8,128)} fusion(bf16[1024,768]{1,0:T(8,128)(2,1)S(1)} %copy-done, f32[1024,3072]{1,0:T(8,128)} %get-tuple-element.50, bf16[1024,768]{1,0:T(8,128)(2,1)S(1)} %fusion.32, bf16[2,3072,768]{2,1,0:T(8,128)(2,1)} %param.15), kind=kOutput, calls=%fused_computation.37 | convolution fusion | flops 9695133696 | bytes 29884416 | tf_op jit(solution)/shard_map/td,tf->df/dot_general | solution.py:48
  78.8 10.3 %fusion.40 = f32[3072,768]{1,0:T(8,128)} fusion(bf16[1024,3072]{1,0:T(8,128)(2,1)} %copy-done.17, bf16[1024,768]{1,0:T(8,128)(2,1)S(1)} %fusion.32), kind=kOutput, calls=%fused_computation.40 | convolution fusion | flops 4831838208 | bytes 17301504 | tf_op jit(solution)/shard_map/tf,td->fd/dot_general | solution.py:46
  89.2 7.7 %fusion.41 = f32[768,3072]{1,0:T(8,128)} fusion(bf16[1024,768]{1,0:T(8,128)(2,1)S(1)} %copy-done.16, bf16[1024,3072]{1,0:T(8,128)(2,1)S(1)} %copy-done.14), kind=kOutput, calls=%fused_computation.41 | convolution fusion | flops 4831838208 | bytes 17301504 | tf_op jit(solution)/shard_map/td,tf->df/dot_general | solution.py:44
  96.8 123.4 %reduce_update.1 = (bf16[2,6,3072]{2,1,0:T(8,128)(2,1)}, bf16[2,24,768]{2,1,0:T(8,128)(2,1)}, f32[6,2,3072]{2,1,0:T(2,128)}, f32[2,24,768]{2,1,0:T(8,128)}, f32[...) custom-call(f32[4,4,48,3072]{3,2,1,0:T(8,128)} %bitcast.56, ...), custom_call_target="tpu_custom_call" | custom-call | tf_op jit(solution)/shard_map/reduce_update/pallas_call | solution.py:392
  220.2 0.9 copy-done.8
  221.1 0.9 copy-done.9
  222.0 57.0 %gather_weights.1 = (bf16[2,4,4,48,3072]{4,3,2,1,0:T(8,128)(2,1)S(1)}, bf16[2,4,4,4,48,768]{5,4,3,2,1,0:T(8,128)(2,1)S(1)}) custom-call(bf16[2,6,3072]{2,1,0:T(8,128)(2,1)S(1)} %copy-done.8, bf16[2,24,768]{2,1,0:T(8,128)(2,1)S(1)} %copy-done.9), custom_call_target="tpu_custom_call" | custom-call | tf_op jit(solution)/shard_map/gather_weights/pallas_call | solution.py:569
  279.0 0.0 copy-start.1
  279.0 1.0 copy-done.2
  280.1 0.9 copy-done.3
  281.0 0.9 copy-done.4
  281.9 0.9 copy-done.5
  282.8 0.9 copy-done.6
  283.7 0.9 copy-done.7
  284.6 0.7 copy-done.10
  285.3 7.0 %finish.1 = (bf16[2,4,4,48,3072]{4,3,2,1,0:T(8,128)(2,1)}, bf16[2,4,4,4,48,768]{5,4,3,2,1,0:T(8,128)(2,1)}, f32[6,2,3072]{2,1,0:T(2,128)}, f32[2,24,768]{2,1,0:T...) custom-call(bf16[2,4,4,48,3072]{4,3,2,1,0:T(8,128)(2,1)S(1)} %get-tu, ...), custom_call_target="tpu_custom_call" | custom-call | tf_op jit(solution)/shard_map/finish/pallas_call | solution.py:597
  292.3 0.5 slice.21
  (24 shorter events, 0.0 us)
Async XLA Ops:
  0.6 1.4 copy-start
  2.1 15.4 %copy-start.11 = (bf16[2,3072,768]{2,1,0:T(8,128)(2,1)S(1)}, bf16[2,3072,768]{2,1,0:T(8,128)(2,1)}, u32[]{:S(2)}) copy-start(bf16[2,3072,768]{2,1,0:T(8,128)(2,1)} %param.15) | copy-start | bytes 28311556
  2.1 21.6 %slice-start = ((s8[9437184]{0:T(1024)(128)(4,1)}), s8[4194304]{0:T(1024)(128)(4,1)S(1)}, s32[]{:S(2)}) async-start(s8[9437184]{0:T(1024)(128)(4,1)} %bitcast.62), calls=%async_computation | async-start | bytes 8388608
  2.1 21.6 %slice-start.1 = ((s8[9437184]{0:T(1024)(128)(4,1)}), s8[4194304]{0:T(1024)(128)(4,1)S(1)}, s32[]{:S(2)}) async-start(s8[9437184]{0:T(1024)(128)(4,1)} %bitcast.62), calls=%async_computation.1 | async-start | bytes 8388608
  14.9 2.6 copy-start.17
  17.5 6.2 %slice-start.2 = ((s8[9437184]{0:T(1024)(128)(4,1)}), s8[1048576]{0:T(1024)(128)(4,1)S(1)}, s32[]{:S(2)}) async-start(s8[9437184]{0:T(1024)(128)(4,1)} %bitcast.62), calls=%async_computation.2 | async-start | bytes 2097152
  22.6 1.1 copy-start.15
  23.7 7.9 %copy-start.12 = (bf16[1024,768]{1,0:T(8,128)(2,1)S(1)}, bf16[1024,768]{1,0:T(8,128)(2,1)}, u32[]{:S(2)}) copy-start(bf16[1024,768]{1,0:T(8,128)(2,1)} %param.13) | copy-start | bytes 4718596
  43.9 13.4 %copy-start.13 = (bf16[1024,3072]{1,0:T(8,128)(2,1)}, bf16[1024,3072]{1,0:T(8,128)(2,1)S(1)}, u32[]{:S(2)}) copy-start(bf16[1024,3072]{1,0:T(8,128)(2,1)S(1)} %fusion.5) | copy-start | bytes 18874372
  78.8 10.3 %copy-start.14 = (bf16[1024,3072]{1,0:T(8,128)(2,1)S(1)}, bf16[1024,3072]{1,0:T(8,128)(2,1)}, u32[]{:S(2)}) copy-start(bf16[1024,3072]{1,0:T(8,128)(2,1)} %copy-done.13) | copy-start | bytes 18874372
  78.8 10.4 %copy-start.16 = (bf16[1024,768]{1,0:T(8,128)(2,1)S(1)}, bf16[1024,768]{1,0:T(8,128)(2,1)}, u32[]{:S(2)}) copy-start(bf16[1024,768]{1,0:T(8,128)(2,1)} %copy-done.15) | copy-start | bytes 4718596
  220.2 0.9 copy-start.8
  221.1 0.9 copy-start.9
  279.0 13.8 %copy-start.1 = (bf16[1024,768]{1,0:T(8,128)(2,1)S(1)}, bf16[1024,768]{1,0:T(8,128)(2,1)}, u32[]{:S(2)}) copy-start(bf16[1024,768]{1,0:T(8,128)(2,1)} %param.12) | copy-start | bytes 4718596
  279.0 1.0 copy-start.2
  280.1 0.9 copy-start.3
  281.0 0.9 copy-start.4
  281.9 0.9 copy-start.5
  282.8 0.9 copy-start.6
  283.7 0.9 copy-start.7
  284.6 0.7 copy-start.10
where the time goes:
time: 293 us
  Pallas kernels  187 us (64%)
  matrix products  90.9 us (31%)
  local copies, waits for them, and re-layouts  12.3 us (4%)
    pallas_call x1, Pallas kernels, reduce_update(): pl.pallas_call(functools.partial(reduce_update_kernel, units, events), ou...  123 us
    pallas_call x1, Pallas kernels, gather_weights(): pl.pallas_call(functools.partial(gather_kernel, units, events), out_shape...  57 us
    dot_general x1, matrix products, local_grads(): jnp.einsum('td,tf->df', act_in, dz_one, preferred_element_type=jnp.float32)  16.5 us
    dot_general x1, matrix products, local_grads(): jnp.einsum('tf,td->fd', act_three, grad_out, preferred_element_type=jnp.f...  13.4 us
    dot_general x1, matrix products, local_grads(): jnp.einsum('td,df->tf', act_in, w_up[0], preferred_element_type=jnp.float32)  12.8 us
    dot_general x1, matrix products, local_grads(): jnp.einsum('td,fd->tf', grad_out, w_down[1], preferred_element_type=jnp.f...  12.2 us
    unnamed x42, local copies, waits for them, and re-layouts  11.8 us
    dot_general x1, matrix products, local_grads(): jnp.einsum('tf,td->fd', act_one, d_hidden, preferred_element_type=jnp.flo...  10.3 us

commit v1 on v0

v1 whole, which is shorter than its diff:
```python
import functools
import math

import jax
import jax.numpy as jnp
from jax import lax
from jax.experimental import pallas as pl
from jax.experimental.pallas import tpu as pltpu
from jax.sharding import PartitionSpec as P

STEP = 10
BETA_ONE = 0.9
BETA_TWO = 0.95
ADAM_EPS = 1e-8
NORM_EPS = 1e-6
INV_SQRT_TWO = 0.7071067811865476
INV_SQRT_TWO_PI = 0.3989422804014327

MESH = pl.DeviceIdType.MESH
RING = 4
ROWS = 48
HALF = 24
LANES = 128
PAIR = 2
PHASES = 3
SENDS = 6
F32 = jnp.float32
BF16 = jnp.bfloat16


def gelu_parts(pre_act):
    normal_cdf = 0.5 * (1.0 + lax.erf(pre_act * INV_SQRT_TWO))
    normal_pdf = jnp.exp(-0.5 * pre_act * pre_act) * INV_SQRT_TWO_PI
    return pre_act * normal_cdf, normal_cdf + pre_act * normal_pdf


def forward(act_in, w_up, w_down):
    z_one = jnp.einsum("td,df->tf", act_in, w_up[0], preferred_element_type=jnp.float32)
    gelu_one, slope_one = gelu_parts(z_one)
    act_one = gelu_one.astype(jnp.bfloat16)
    hidden = jnp.einsum("tf,fd->td", act_one, w_down[0], preferred_element_type=jnp.float32).astype(jnp.bfloat16)
    z_three = jnp.einsum("td,df->tf", hidden, w_up[1], preferred_element_type=jnp.float32)
    gelu_three, slope_three = gelu_parts(z_three)
    return act_one, slope_one, hidden, gelu_three.astype(jnp.bfloat16), slope_three


def adam_direction(exp_avg, exp_sq, grad, clip_scale):
    bias_one = 1.0 - BETA_ONE ** STEP
    bias_two = 1.0 - BETA_TWO ** STEP
    avg_new = BETA_ONE * exp_avg + (1.0 - BETA_ONE) * clip_scale * grad
    sq_new = BETA_TWO * exp_sq + (1.0 - BETA_TWO) * (clip_scale * clip_scale) * (grad * grad)
    direction = (avg_new / bias_one) / (jnp.sqrt(sq_new / bias_two) + ADAM_EPS)
    return avg_new, sq_new, direction


class Unit:
    def __init__(self, kind, k, off, cols, order):
        self.kind, self.k, self.off, self.cols, self.order = kind, k, off, cols, order
        self.dims = "zy" if kind == "up" else "zyx"
        self.shape = (RING,) * len(self.dims) + (ROWS, cols)

    def half(self, phase, dest, h, me):
        if self.kind == "up" and phase == 2:
            return (dest, h), (6, self.cols)
        fixed = {d: me[d] for d in self.order[:phase]}
        fixed[self.order[phase]] = dest
        index, shape, split = [], [], False
        for d in self.dims:
            if d in fixed:
                index.append(fixed[d])
            elif not split:
                index.append(pl.ds(PAIR * h, 2))
                shape.append(2)
                split = True
            else:
                index.append(slice(None))
                shape.append(RING)
        if split:
            return tuple(index), tuple(shape) + (ROWS, self.cols)
        return tuple(index) + (pl.ds(HALF * h, HALF),), (HALF, self.cols)

    def half_shape(self, phase):
        return self.half(phase, 0, 0, dict(x=0, y=0, z=0))[1]


def make_units(up_cols, down_cols):
    u, d = up_cols // PAIR, down_cols // 3
    return [
        Unit("down", 1, 0, PAIR * d, "xyz"),
        Unit("down", 1, PAIR * d, d, "xzy"),
        Unit("up", 1, 0, u, "zyx"),
        Unit("up", 1, u, u, "yzx"),
        Unit("up", 0, 0, u, "zyx"),
        Unit("up", 0, u, u, "yzx"),
        Unit("down", 0, 0, d, "xyz"),
        Unit("down", 0, d, d, "yzx"),
        Unit("down", 0, PAIR * d, d, "zxy"),
    ]


def serve_order(slots, ready, phases, tail, moved_per_us):
    rate, hop = 43000.0, 3.0
    link, now, plan = {}, 0.0, []
    ready, state, late = list(ready), [0] * len(ready), [0.0] * len(ready)
    ends = [PAIR * len(p) + tail for p in phases]

    def send(phase):
        d, nbytes = phase
        for sign in "+-":
            link[d, sign] = max(link.get((d, sign), 0.0), now) + nbytes / rate
        return max(link[d, sign] for sign in "+-") + hop

    for duration, starts in list(slots) + [(None, ())]:
        served = []
        while True:
            open_units = [j for j in range(len(ready)) if state[j] <= ends[j] and ready[j] is not None]
            if not open_units:
                break
            i = min(open_units, key=lambda j: (ready[j], j))
            if duration is not None and ready[i] > now:
                break
            phase, middle = divmod(state[i], 2)
            served.append((i, state[i]))
            now = max(now, ready[i])
            if state[i]:
                now += 0.3 + 8 * phases[i][(state[i] - 1) // PAIR if state[i] <= PAIR * len(phases[i]) else -1][1] / moved_per_us
            if phase < len(phases[i]):
                ready[i] = send(phases[i][phase])
                if middle:
                    ready[i] = max(ready[i], late[i])
                else:
                    late[i] = send(phases[i][phase])
            else:
                ready[i] = now + hop
            state[i] += 1
        plan.append(served)
        if duration is not None:
            now += duration
            for i in starts:
                ready[i] = now
    return plan


def half_bytes(shape, dtype):
    return math.prod(shape) * jnp.dtype(dtype).itemsize


def position():
    me = lax.axis_index("data")
    return dict(z=me // 32, y=(me // 8) % RING, x=(me // PAIR) % RING, c=me % PAIR)


def device_of(at):
    return (((at["z"] * RING + at["y"]) * RING + at["x"]) * 2 + at["c"],)


def moved(me, d, by):
    return device_of({**me, d: (me[d] + by) % RING})


def partner_of(me):
    return device_of({**me, "c": 1 - me["c"]})


def group_peers(me):
    first, second = [], []
    j, q = me["x"] * 2 + me["c"], me["z"] * 4 + me["y"]
    for t in range(1, 8):
        o = (j + t) % 8
        first.append((o, device_of({**me, "x": o // PAIR, "c": o % PAIR})))
    for t in range(1, 16):
        o = (q + t) % 16
        second.append((o, device_of({**me, "z": o // 4, "y": o % RING})))
    return first, second


def remote(src, dst, send_sem, recv_sem, device):
    return pltpu.make_async_remote_copy(src_ref=src, dst_ref=dst, send_sem=send_sem, recv_sem=recv_sem, device_id=device, device_id_type=MESH)


def add_into(dst, *srcs):
    lead = dst.shape[:-2]
    if not lead:
        dst[...] = functools.reduce(lambda a, b: a + b, [s[...] for s in srcs], dst[...])
        return

    def body(i, carry):
        index = []
        for n in reversed(lead):
            index.append(i % n)
            i = i // n
        index = tuple(reversed(index))
        dst[index] = functools.reduce(lambda a, b: a + b, [s[index] for s in srcs], dst[index])
        return carry

    lax.fori_loop(0, math.prod(lead), body, 0)


def dot(a, b, contract):
    return lax.dot_general(a, b, ((contract[:1], contract[1:]), ((), ())), preferred_element_type=F32)


def grad_update_kernel(units, plan, *refs):
    take = iter(refs)
    act_in, grad_out, hidden, act_one, act_three, slope_one, slope_three, w_up, w_down = [next(take) for _ in range(9)]
    master = dict(up=next(take), down=next(take))
    avg = dict(up=next(take), down=next(take))
    sq = dict(up=next(take), down=next(take))
    rate_ref, clip_ref = next(take), next(take)
    weight = dict(up=next(take), down=next(take))
    master_out = dict(up=next(take), down=next(take))
    avg_out = dict(up=next(take), down=next(take))
    sq_out = dict(up=next(take), down=next(take))
    norm_ref = next(take)
    acc_up = next(take)
    acc = [acc_up.at[1 - u.k, int(u.off > 0)] if u.kind == "up" else next(take) for u in units]
    recv = [[[next(take) for _ in range(SENDS)] for _ in range(PHASES)] for _ in units]
    xbuf = {i: next(take) for i, u in enumerate(units) if u.kind == "up"}
    fin = [next(take) for _ in units]
    grad = dict(up=next(take), down=next(take))
    small_src, small_one, small_two = next(take), next(take), next(take)
    stage_down, stage_up, inner, right, outer, w_tile, s_tile, a_tile, w_wide = [next(take) for _ in range(9)]
    down_send, down_recv, up_send, up_recv, ring_send, ring_recv, fin_send, fin_recv = [next(take) for _ in range(8)]
    one_send, one_recv, two_send, two_recv = [next(take) for _ in range(4)]
    w_sem, s_sem, a_sem, load_sem = [next(take) for _ in range(4)]

    me = position()
    core = me["c"]
    partner = partner_of(me)
    first, second = group_peers(me)
    n_tiles, piece_cols, wide = 12, w_tile.shape[1], a_tile.shape[2]
    down_half = grad["down"].shape[-1] // PAIR

    load_right = pltpu.make_async_copy(grad_out, right, load_sem.at[0])
    load_outer = pltpu.make_async_copy(hidden, outer, load_sem.at[1])
    load_next = pltpu.make_async_copy(act_in, outer, load_sem.at[1])

    def load_wide(n):
        rows = pl.ds(pl.multiple_of(n * piece_cols, piece_cols), piece_cols)
        return pltpu.make_async_copy(w_up.at[1, rows], w_wide, load_sem.at[2])

    def load_a(source, t):
        return pltpu.make_async_copy(source.at[:, pl.ds(pl.multiple_of(t % 8 * wide, LANES), wide)], a_tile.at[t % PAIR], a_sem.at[t % PAIR])

    def tile_columns(t):
        half = jnp.where(t < n_tiles // PAIR, 1 - core, core)
        return pl.ds(pl.multiple_of((half * (n_tiles // PAIR) + t % (n_tiles // PAIR)) * piece_cols, piece_cols), piece_cols)

    def load_tile(at, wait):
        stage, slot, cols = at // n_tiles, at % PAIR, tile_columns(at % n_tiles)
        w_copy = pltpu.make_async_copy(w_down.at[1 - stage, cols], w_tile.at[slot], w_sem.at[slot])
        if wait:
            w_copy.wait()
            pltpu.make_async_copy(slope_one.at[:, cols], s_tile.at[slot], s_sem.at[slot]).wait()
            return
        w_copy.start()
        for n, source in enumerate((slope_three, slope_one)):
            pl.when(stage == n)(pltpu.make_async_copy(source.at[:, cols], s_tile.at[slot], s_sem.at[slot]).start)

    load_right.start()
    load_a(act_three, 0).start()
    load_outer.start()
    load_tile(0, False)
    load_wide(0).start()

    barrier = pltpu.get_barrier_semaphore()
    for _, device in first + second:
        pl.semaphore_signal(barrier, inc=1, device_id=device, device_id_type=MESH)
    pl.semaphore_wait(barrier, len(first) + len(second))

    sent = []

    def ring(i, phase, n):
        u = units[i]
        d = u.order[phase]
        base = xbuf[i] if u.kind == "up" and phase == 2 else acc[i]
        by = 1 if n % PAIR == 0 else -1
        dest = (me[d] + (2 if n < 2 else by)) % RING
        h = (0, 1, 1, 0, 0, 1)[n]
        src = base.at[u.half(phase, dest, h, me)[0]]
        s = (i * PHASES + phase) * SENDS + n
        return remote(src, recv[i][phase][n], ring_send.at[s], ring_recv.at[s], moved(me, d, by))

    def last_piece(i, c):
        u = units[i]
        if u.kind == "up":
            return xbuf[i].at[me["x"], c]
        return acc[i].at[me["z"], me["y"], me["x"], pl.ds(pl.multiple_of(HALF * c, 8), HALF)]

    def swap(i):
        return remote(last_piece(i, 1 - core), fin[i], fin_send.at[i], fin_recv.at[i], partner)

    def send(make):
        make().start()
        sent.append(make)

    def start_phase(i, phase):
        u = units[i]
        if u.kind == "up" and phase == 2:
            block = acc[i][me["z"], me["y"]]
            for p in range(8):
                xbuf[i][p // PAIR, p % PAIR] = block[6 * p:6 * p + 6]
        for n in range(4):
            send(functools.partial(ring, i, phase, n))

    def serve(i, s):
        u = units[i]
        if s == 0:
            start_phase(i, 0)
        elif s < 7 and s % PAIR == 1:
            phase = (s - 1) // PAIR
            d = u.order[phase]
            base = xbuf[i] if u.kind == "up" and phase == 2 else acc[i]
            for n in (4, 5):
                ring(i, phase, n - 4).wait_recv()
                dest = (me[d] + (1 if n == 4 else -1)) % RING
                add_into(base.at[u.half(phase, dest, n - 4, me)[0]], recv[i][phase][n - 4])
                send(functools.partial(ring, i, phase, n))
        elif s < 7:
            phase = s // PAIR - 1
            d = u.order[phase]
            base = xbuf[i] if u.kind == "up" and phase == 2 else acc[i]
            for n in (PAIR, 3, 4, 5):
                ring(i, phase, n).wait_recv()
            for h, (a, b) in enumerate(((4, 3), (PAIR, 5))):
                add_into(base.at[u.half(phase, me[d], h, me)[0]], recv[i][phase][a], recv[i][phase][b])
            if phase < 2:
                start_phase(i, phase + 1)
            else:
                send(functools.partial(swap, i))
        else:
            swap(i).wait_recv()
            own, other = last_piece(i, core)[...], fin[i][...]
            half = grad[u.kind].shape[-1] // PAIR
            grad[u.kind][u.k, :, u.off:u.off + u.cols] = jnp.where(core == 0, own, other) * (1.0 / 128.0)
            grad[u.kind][u.k, :, half + u.off:half + u.off + u.cols] = jnp.where(core == 0, other, own) * (1.0 / 128.0)

    def serve_at(t, steps):
        if steps:
            @pl.when(t[0] == t[1])
            def _():
                for i, s in steps:
                    serve(i, s)

    def down_piece(i, z):
        u = units[i]
        return remote(stage_down.at[z, :, :, :, u.off:u.off + u.cols], acc[i].at[z], down_send.at[i, z], down_recv.at[i, z], partner)

    def down_grad(source, following, group, steps):
        def tile(t, carry):
            for k, served in enumerate(steps):
                serve_at((t, k), served)
            load_a(source, t).wait()
            pl.when(t < 15)(lambda: load_a(source, t + 1).start())
            if following is not None:
                pl.when(t == 15)(lambda: load_a(following, 0).start())
            columns = jnp.where(t < 8, 1 - core, core)
            value = dot(a_tile[t % PAIR], right[:, pl.ds(pl.multiple_of(columns * down_half, LANES), down_half)], (0, 0))
            value = value.reshape(PAIR, RING, ROWS, down_half)
            z, y = t % 8 // PAIR, pl.ds(t % PAIR * 2, 2)

            @pl.when(t < 8)
            def _():
                stage_down[z, y] = value
                pl.when(t % PAIR == 1)(lambda: [down_piece(i, z).start() for i in group] and None)

            @pl.when(t >= 8)
            def _():
                pl.when(t % PAIR == 0)(lambda: [down_piece(i, z).wait_recv() for i in group] and None)
                for i in group:
                    acc[i][z, y] += value[..., units[i].off:units[i].off + units[i].cols]
            return carry

        lax.fori_loop(0, 16, tile, 0)

    def up_piece(n):
        cols = pl.ds(pl.multiple_of(n % 3 * piece_cols, piece_cols), piece_cols)
        return remote(stage_up.at[:, :, :, cols], acc_up.at[n // 6, n // 3 % PAIR, :, :, :, cols], up_send.at[n], up_recv.at[n], partner)

    def up_tile(at, carry):
        for k, steps in enumerate(plan["up"]):
            serve_at((at, k), steps)

        @pl.when(at == n_tiles)
        def _():
            load_next.start()
            for n in range(PHASES):
                load_wide(n).wait()
                right[:, n * piece_cols:(n + 1) * piece_cols] = dot(inner[...], w_wide[...], (1, 1)).astype(BF16)
                if n < 2:
                    load_wide(n + 1).start()
            load_next.wait()

        load_tile(at, True)
        pl.when(at < PAIR * n_tiles - 1)(lambda: load_tile(at + 1, False))
        stage, t = at // n_tiles, at % n_tiles
        cols = tile_columns(t)
        inner[:, cols] = (dot(right[...], w_tile[at % PAIR], (1, 1)) * s_tile[at % PAIR]).astype(BF16)
        n = stage * 6 + t % 6
        place = pl.ds(pl.multiple_of(t % 3 * piece_cols, piece_cols), piece_cols)
        pl.when((t < 6) & (n > 2))(lambda: up_piece(n - 3).wait_send())
        pl.when(t >= 6)(lambda: up_piece(n).wait_recv())
        rows = outer.shape[1] // PAIR
        for r in range(2):
            value = dot(outer[:, r * rows:(r + 1) * rows], inner[:, cols], (0, 0)).reshape(PAIR, RING, ROWS, piece_cols)

            @pl.when(t < 6)
            def _():
                stage_up[PAIR * r:PAIR * r + 2, :, :, place] = value

            @pl.when(t >= 6)
            def _():
                acc_up[stage, t // 3 % PAIR, PAIR * r:PAIR * r + 2, :, :, place] += value
        pl.when(t < 6)(lambda: up_piece(n).start())
        return carry

    load_right.wait()
    down_grad(act_three, act_one, (0, 1), ())
    load_outer.wait()
    lax.fori_loop(0, PAIR * n_tiles, up_tile, 0)
    for i in (0, 1):
        for z in range(RING):
            down_piece(i, z).wait_send()
    down_grad(act_one, None, (6, 7, 8), plan["down"])
    for i, s in plan["end"]:
        serve(i, s)

    def total(values):
        row = lax.broadcasted_iota(jnp.int32, (8, LANES), 0)
        tile = jnp.zeros((8, LANES), F32)
        for r, value in enumerate(values):
            tile = jnp.where(row == r, value, tile)
        return tile

    def all_sum(at, tile):
        for stage, (peers, own, buf, send_s, recv_s) in enumerate((
            (first, me["x"] * 2 + core, small_one, one_send, one_recv),
            (second, me["z"] * RING + me["y"], small_two, two_send, two_recv),
        )):
            small_src[at, stage] = tile
            buf[at, own] = tile
            for t, (o, device) in enumerate(peers):
                send(functools.partial(remote, small_src.at[at, stage], buf.at[at, own], send_s.at[at, t], recv_s.at[at, own], device))
            for o, device in peers:
                remote(small_src.at[at, stage], buf.at[at, o], send_s.at[at, 0], recv_s.at[at, o], device).wait_recv()
            tile = buf[at, 0]
            for o in range(1, len(peers) + 1):
                tile = tile + buf[at, o]
        return tile

    def squares(x):
        return jnp.sum(x * x)

    def rows(kind, k):
        return (slice(None), k) if kind == "up" else (k,)

    keys = (("up", 0), ("down", 0), ("up", 1), ("down", 1))
    local_sq = functools.reduce(lambda a, b: a + b, [squares(grad[kind][k]) for kind, k in keys])
    sums = all_sum(0, total([local_sq] + [squares(master[kind][rows(kind, k)]) for kind, k in keys]))
    norm = jnp.sqrt(sums[0:1, :])
    norm_ref[...] = jnp.broadcast_to(norm, norm_ref.shape)
    clip_scale = jnp.minimum(1.0, clip_ref[0] / (norm + NORM_EPS))[:, 0:1]
    master_norm = jnp.sqrt(sums)
    local = []
    for kind, k in keys:
        avg_new, sq_new, direction = adam_direction(avg[kind][rows(kind, k)], sq[kind][rows(kind, k)], grad[kind][k], clip_scale)
        avg_out[kind][rows(kind, k)] = avg_new
        sq_out[kind][rows(kind, k)] = sq_new
        grad[kind][k] = direction
        local.append(squares(direction))
    dir_norm = jnp.sqrt(all_sum(1, total(local)))
    for r, (kind, k) in enumerate(keys):
        ratio = (master_norm[r + 1:r + 2, :] / dir_norm[r:r + 1, :])[:, 0:1]
        new = master[kind][rows(kind, k)] - rate_ref[0] * ratio * grad[kind][k]
        master_out[kind][rows(kind, k)] = new
        weight[kind][k] = new.astype(BF16)

    for i in (6, 7, 8):
        for z in range(RING):
            down_piece(i, z).wait_send()
    for n in range(9, 12):
        up_piece(n).wait_send()
    for make in sent:
        make().wait_send()


def grad_update(tensors, master, avg, sq, learn_rate, clip_norm):
    tokens, down_cols = tensors[0].shape
    up_cols = tensors[3].shape[1]
    units = make_units(up_cols // PAIR, down_cols // PAIR)
    phases = [[(u.order[p], half_bytes(u.half_shape(p), F32)) for p in range(PHASES)] for u in units]
    slots = [(12.0, (0, 1))]
    slots += [(1.3 + (t == 11) * 7, {8: (2,), 11: (3,), 20: (4,), 23: (5,)}.get(t, ())) for t in range(24)]
    slots += [(0.75, (6, 7, 8) if t == 15 else ()) for t in range(16)]
    steps = serve_order(slots, [None] * len(units), phases, 1, 1500000.0)
    plan = dict(up=steps[1:25], down=steps[25:41], end=steps[41])
    master, avg, sq = [(up.transpose(1, 0, 2), down) for up, down in (master, avg, sq)]
    blocks = [(PAIR, 6, up_cols), (PAIR, HALF, down_cols)]
    piece = up_cols // 12
    scratch = [pltpu.VMEM((PAIR, 2, RING, RING, ROWS, up_cols // RING), F32)]
    scratch += [pltpu.VMEM(u.shape, F32) for u in units if u.kind == "down"]
    scratch += [pltpu.VMEM(u.half_shape(p), F32) for u in units for p in range(PHASES) for _ in range(SENDS)]
    scratch += [pltpu.VMEM((RING, 2, 6, u.cols), F32) for u in units if u.kind == "up"]
    scratch += [pltpu.VMEM((6 if u.kind == "up" else HALF, u.cols), F32) for u in units]
    scratch += [pltpu.VMEM(b, F32) for b in blocks]
    scratch += [pltpu.VMEM((PAIR, 2, 8, LANES), F32), pltpu.VMEM((PAIR, 8, 8, LANES), F32), pltpu.VMEM((PAIR, 16, 8, LANES), F32)]
    scratch += [pltpu.VMEM((RING, RING, RING, ROWS, down_cols // PAIR), F32), pltpu.VMEM((RING, RING, ROWS, 3 * piece), F32)]
    scratch += [pltpu.VMEM((tokens, up_cols), BF16), pltpu.VMEM((tokens, down_cols), BF16), pltpu.VMEM((tokens, down_cols), BF16)]
    scratch += [pltpu.VMEM((PAIR, piece, down_cols), BF16), pltpu.VMEM((PAIR, tokens, piece), F32)]
    scratch += [pltpu.VMEM((PAIR, tokens, up_cols // 8), BF16), pltpu.VMEM((piece, up_cols), BF16)]
    n = len(units)
    dma = pltpu.SemaphoreType.DMA
    scratch += [dma((n, RING)), dma((n, RING)), dma((12,)), dma((12,)), dma((n * PHASES * SENDS,)), dma((n * PHASES * SENDS,)), dma((n,)), dma((n,))]
    scratch += [dma((PAIR, 7)), dma((PAIR, 8)), dma((PAIR, 15)), dma((PAIR, 16)), dma((2,)), dma((2,)), dma((2,)), dma((3,))]
    vmem, smem, any_space = [pl.BlockSpec(memory_space=s) for s in (pltpu.VMEM, pltpu.SMEM, pl.ANY)]
    state = [jax.ShapeDtypeStruct(a.shape, F32) for a in master]
    return pl.pallas_call(
        functools.partial(grad_update_kernel, units, plan),
        out_shape=[jax.ShapeDtypeStruct(b, BF16) for b in blocks] + state * 3 + [jax.ShapeDtypeStruct((8, LANES), F32)],
        in_specs=[any_space] * len(tensors) + [vmem] * 6 + [smem] * 2,
        out_specs=[vmem] * 9,
        scratch_shapes=scratch,
        compiler_params=pltpu.CompilerParams(collective_id=0, has_side_effects=True, vmem_limit_bytes=67043328),
        name="grad_update",
    )(*tensors, *master, *avg, *sq, learn_rate.reshape(1), clip_norm.reshape(1))


class Gather:
    def __init__(self, kind, k, off, cols, order):
        self.kind, self.k, self.off, self.cols, self.order = kind, k, off, cols, order
        self.dims = "zy" if kind == "up" else "zyx"
        self.shape = (RING,) * len(self.dims) + (ROWS, cols)

    def chunk(self, phase, owner, me, h=None):
        gathered, d = self.order[:phase], self.order[phase]
        index, shape, split = [], [], h is None
        for e in self.dims:
            if e == d:
                index.append(owner)
            elif e not in gathered:
                index.append(me[e])
            elif split:
                index.append(slice(None))
                shape.append(RING)
            else:
                index.append(pl.ds(PAIR * h, 2))
                shape.append(2)
                split = True
        if split:
            return tuple(index), tuple(shape) + (ROWS, self.cols)
        return tuple(index) + (pl.ds(HALF * h, HALF),), (HALF, self.cols)


def make_gathers(up_cols, down_cols):
    u, d = up_cols // PAIR, down_cols // 3
    return [
        Gather("down", 1, 0, PAIR * d, "zyx"),
        Gather("down", 0, 0, PAIR * d, "yzx"),
        Gather("down", 1, PAIR * d, d, "xzy"),
        Gather("down", 0, PAIR * d, d, "xyz"),
        Gather("up", 1, 0, u, "yz"),
        Gather("up", 1, u, u, "zy"),
        Gather("up", 0, 0, u, "yz"),
        Gather("up", 0, u, u, "zy"),
    ]


def gather_kernel(units, events, up_ref, down_ref, out_up, out_down, *refs):
    take = iter(refs)
    block = [next(take) for _ in units]
    rows_up, rows_down, assembly = next(take), next(take), next(take)
    row_send, row_recv, core_send, core_recv, ring_send, ring_recv, own_sem, share_send, share_recv = [next(take) for _ in range(9)]
    me = position()
    core = me["c"]
    partner = partner_of(me)
    own = me["x"] * 2 + core
    first = group_peers(me)[0]
    around = [moved(me, d, by) for d in "zy" for by in (1, -1)]
    half_up, half_down = up_ref.shape[-1] // PAIR, down_ref.shape[-1] // PAIR

    barrier = pltpu.get_barrier_semaphore()
    for device in [device for _, device in first] + around:
        pl.semaphore_signal(barrier, inc=1, device_id=device, device_id_type=MESH)
    pl.semaphore_wait(barrier, len(first) + len(around))

    sent = []

    def send(copy):
        copy.start()
        sent.append(copy)

    other = pl.ds(pl.multiple_of((1 - core) * half_down, LANES), half_down)
    core_copy = remote(down_ref.at[:, :, other], rows_down, core_send, core_recv, partner)
    send(core_copy)
    for t, (o, device) in enumerate(first):
        width = pl.ds(pl.multiple_of((o % PAIR) * half_up, LANES), half_up)
        send(remote(up_ref.at[:, :, width], rows_up.at[own], row_send.at[t], row_recv.at[own], device))

    def part(i, phase, owner, h=None, of=core):
        u = units[i]
        out, half = (out_up, half_up) if u.kind == "up" else (out_down, half_down)
        at = u.chunk(phase, owner, me, h)[0]
        at = at + (slice(None),) * (len(u.dims) + 1 - len(at))
        return out.at[(u.k,) + at + (pl.ds(pl.multiple_of(of * half + u.off, LANES), u.cols),)]

    def ring(i, phase, n):
        d = units[i].order[phase]
        by = 1 if n % PAIR == 0 else -1
        owner = me[d] if n < 4 else (me[d] - by) % RING
        ref = part(i, phase, owner, (0, 1, 1, 0, 0, 1)[n])
        s = (i * PHASES + phase) * SENDS + n
        return remote(ref, ref, ring_send.at[s], ring_recv.at[s], moved(me, d, by))

    def start_phase(i, phase):
        for n in range(4):
            send(ring(i, phase, n))

    shares = []

    def share(i, j, owner):
        phase = len(units[i].order) - 1
        mine, theirs = part(i, phase, owner), part(i, phase, owner, None, 1 - core)
        send(remote(mine, mine, share_send.at[i, j], share_recv.at[i, j], partner))
        shares.append(remote(theirs, theirs, share_send.at[i, j], share_recv.at[i, j], partner))

    rows_ready = [False]
    for i, s in events:
        u = units[i]
        last = len(u.order) - 1
        if s == 0:
            if u.kind == "down":
                if i == 0:
                    core_copy.wait_recv()
                low, high = down_ref[u.k, :, u.off:u.off + u.cols], down_ref[u.k, :, half_down + u.off:half_down + u.off + u.cols]
                mine = jnp.where(core == 0, low, high)
                theirs = rows_down[u.k, :, u.off:u.off + u.cols]
                block[i][...] = jnp.concatenate([jnp.where(core == 0, mine, theirs), jnp.where(core == 0, theirs, mine)], axis=0)
            else:
                if not rows_ready[0]:
                    rows_ready[0] = True
                    rows_up[own] = jnp.where(core == 0, up_ref[:, :, :half_up], up_ref[:, :, half_up:])
                    for o, device in first:
                        remote(rows_up.at[o], rows_up.at[o], row_send.at[0], row_recv.at[o], device).wait_recv()
                for p in range(8):
                    assembly[6 * p:6 * p + 6, :] = rows_up[p, u.k, :, u.off:u.off + u.cols].astype(F32)
                block[i][...] = assembly[...].astype(BF16)
            own_copy = pltpu.make_async_copy(block[i], part(i, 0, me[u.order[0]]), own_sem.at[i])
            own_copy.start()
            own_copy.wait()
            start_phase(i, 0)
        elif s % PAIR == 1:
            phase = (s - 1) // PAIR
            if phase == last:
                share(i, 0, me[u.order[last]])
            for n in (4, 5):
                d = u.order[phase]
                incoming = part(i, phase, (me[d] + (-1 if n == 4 else 1)) % RING, n - 4)
                remote(incoming, incoming, ring_send.at[0], ring_recv.at[(i * PHASES + phase) * SENDS + n - 4], moved(me, d, 1)).wait_recv()
                send(ring(i, phase, n))
        else:
            phase = s // PAIR - 1
            d = u.order[phase]
            for n in (PAIR, 3, 4, 5):
                step = {2: -1, 3: 1, 4: -2, 5: 2}[n]
                h = {2: 1, 3: 0, 4: 0, 5: 1}[n]
                incoming = part(i, phase, (me[d] + step) % RING, h)
                remote(incoming, incoming, ring_send.at[0], ring_recv.at[(i * PHASES + phase) * SENDS + n], moved(me, d, 1)).wait_recv()
                if phase == last and n == 3:
                    share(i, 1, (me[d] - 1) % RING)
                    share(i, 2, (me[d] + 1) % RING)
            if phase < last:
                start_phase(i, phase + 1)
            else:
                share(i, 3, (me[d] + 2) % RING)

    for copy in shares:
        copy.wait_recv()
    for copy in sent:
        copy.wait_send()


def gather_weights(block_up, block_down):
    up_cols, down_cols = block_up.shape[2], block_down.shape[2]
    units = make_gathers(up_cols // PAIR, down_cols // PAIR)
    here = dict(x=0, y=0, z=0)
    phases = [[(d, half_bytes(u.chunk(p, 0, here, 0)[1], BF16)) for p, d in enumerate(u.order)] for u in units]
    events = serve_order((), [2.0 if u.kind == "down" else 6.0 for u in units], phases, 0, math.inf)[0]
    n = len(units)
    dma = pltpu.SemaphoreType.DMA
    scratch = [pltpu.VMEM((ROWS, u.cols), BF16) for u in units]
    scratch += [pltpu.VMEM((8, 2, 6, up_cols // PAIR), BF16), pltpu.VMEM((PAIR, HALF, down_cols // PAIR), BF16), pltpu.VMEM((ROWS, up_cols // 4), F32)]
    scratch += [dma((7,)), dma((8,)), dma, dma, dma((n * PHASES * SENDS,)), dma((n * PHASES * SENDS,)), dma((n,)), dma((n, 4)), dma((n, 4))]
    vmem = pl.BlockSpec(memory_space=pltpu.VMEM)
    out_up, out_down = pl.pallas_call(
        functools.partial(gather_kernel, units, events),
        out_shape=[jax.ShapeDtypeStruct((PAIR, RING, RING, ROWS, up_cols), BF16), jax.ShapeDtypeStruct((PAIR, RING, RING, RING, ROWS, down_cols), BF16)],
        in_specs=[vmem] * 2,
        out_specs=[pl.BlockSpec(memory_space=pl.ANY)] * 2,
        scratch_shapes=scratch,
        compiler_params=pltpu.CompilerParams(collective_id=1, has_side_effects=True, vmem_limit_bytes=HALF * 1024 * 1024),
        name="gather_weights",
    )(block_up, block_down)
    return out_up, out_down


def finish_kernel(*refs):
    n = (len(refs) - 1) // PAIR
    copies = []
    for i in range(n):
        src, dst = refs[i], refs[n + i]
        for j in range(src.shape[0] * 2 if len(src.shape) > 3 else 1):
            at = (j // PAIR, pl.ds(j % PAIR * 2, 2)) if len(src.shape) > 3 else slice(None)
            copies.append(pltpu.make_async_copy(src.at[at], dst.at[at], refs[-1].at[i, j]))
    for copy in copies:
        copy.start()
    for copy in copies:
        copy.wait()


def finish(arrays):
    any_space = pl.BlockSpec(memory_space=pl.ANY)
    return pl.pallas_call(
        finish_kernel,
        out_shape=[jax.ShapeDtypeStruct(a.shape, a.dtype) for a in arrays],
        in_specs=[any_space] * len(arrays),
        out_specs=[any_space] * len(arrays),
        scratch_shapes=[pltpu.SemaphoreType.DMA((len(arrays), 4))],
        compiler_params=pltpu.CompilerParams(vmem_limit_bytes=1024 * 1024),
        name="finish",
    )(*arrays)


def solution(mesh):
    batch_rows = P("data", None)
    state_rows = P(None, "data", None)
    replicated = P()

    def device_step(act_in, grad_out, w_up, w_down, master_up, master_down, exp_avg_up, exp_avg_down, exp_sq_up, exp_sq_down, learn_rate, clip_norm):
        act_one, slope_one, hidden, act_three, slope_three = forward(act_in, w_up, w_down)
        tensors = (act_in, grad_out, hidden, act_one, act_three, slope_one, slope_three, w_up, w_down)
        outs = grad_update(tensors, (master_up, master_down), (exp_avg_up, exp_avg_down), (exp_sq_up, exp_sq_down), learn_rate, clip_norm)
        new_w_up, new_w_down, *state, norm = finish((*gather_weights(*outs[:2]), *outs[2:]))
        state = [a.transpose(1, 0, 2) if i % PAIR == 0 else a for i, a in enumerate(state)]
        return (new_w_up.reshape(w_up.shape), new_w_down.reshape(w_down.shape), *state, norm[0, 0])

    return jax.shard_map(device_step, mesh=mesh, in_specs=(batch_rows, batch_rows, replicated, replicated, state_rows, state_rows, state_rows, state_rows, state_rows, state_rows, replicated, replicated), out_specs=(replicated, replicated, state_rows, state_rows, state_rows, state_rows, state_rows, state_rows, replicated), check_vma=False)
```

time: 293 us -> 286 us (0.976)
  matrix products: 90.9 us -> 29.9 us
  Pallas kernels: 187 us -> 243 us
  local copies, waits for them, and re-layouts: 12.3 us -> 9.32 us
    dot_general x9 -> x3, matrix products: 90.9 us -> 29.9 us  [the longest x1 12.9 us: forward(): jnp.einsum('td,df->tf', hidden, w_up[1], preferred_element_type=jnp.float32)]
    pallas_call x1, Pallas kernels: 123 us -> 178 us  [grad_update(): pl.pallas_call(functools.partial(grad_update_kernel, units, plan), out_sh...]
    unnamed x42 -> x26, local copies, waits for them, and re-layouts: 11.8 us -> 8.81 us
where the time goes in v1:
time: 286 us; the launch traced here: 284 us
  Pallas kernels  243 us (85%)
  matrix products  29.9 us (10%)
  local copies, waits for them, and re-layouts  9.32 us (3%)
    pallas_call x1, Pallas kernels, grad_update(): pl.pallas_call(functools.partial(grad_update_kernel, units, plan), out_sh...  178 us
    pallas_call x1, Pallas kernels, gather_weights(): pl.pallas_call(functools.partial(gather_kernel, units, events), out_shape...  58 us
    dot_general x1, matrix products, forward(): jnp.einsum('td,df->tf', hidden, w_up[1], preferred_element_type=jnp.float32)  12.9 us
    dot_general x1, matrix products, forward(): jnp.einsum('td,df->tf', act_in, w_up[0], preferred_element_type=jnp.float32)  11.9 us
    unnamed x26, local copies, waits for them, and re-layouts  8.81 us
    pallas_call x1, Pallas kernels, finish(): pl.pallas_call(finish_kernel, out_shape=[jax.ShapeDtypeStruct(a.shape, a....  7.01 us

profile of v1, /device:TPU:1, one launch (start us, length us, event | category | flops | bytes accessed | tf_op | source)
XLA Modules:
  0.0 283.9 jit_solution(8210768135210518391)
XLA Ops:
  1.9 0.0 copy-start.10
  1.9 11.9 %fusion.3 = (f32[1024,3072]{1,0:T(8,128)}, bf16[1024,3072]{1,0:T(8,128)(2,1)S(1)}) fusion(bf16[1024,768]{1,0:T(8,128)(2,1)} %refs_0_.1, bf16[2,768,3072]{2,1,0:T(8,128)(2,1)} %refs_7_.1), kind=kOutput, calls=%fused_computation.5 | convolution fusion | flops 4863295488 | bytes 25165824 | tf_op jit(solution)/shard_map/td,df->tf/dot_general | solution.py:38
  13.9 0.0 copy-done.10
  13.9 0.0 copy-start.9
  13.9 5.0 %fusion.10.refs_2_ = bf16[1024,768]{1,0:T(8,128)(2,1)S(1)} fusion(bf16[1024,3072]{1,0:T(8,128)(2,1)S(1)} %get-tuple-element.52.refs_3_, bf16[2,3072,768]{2,1,0:T(8,128)(2,1)S(1)} %copy-done.10), kind=kOutput, calls=%fused_computation.16 | convolution fusion | flops 4831838208 | bytes 12582912 | tf_op jit(solution)/shard_map/tf,fd->td/dot_general | solution.py:41
  18.9 0.0 copy-done.11
  19.0 0.9 copy-done.9
  19.9 0.0 copy-start.12
  19.9 12.9 %fusion.7 = (f32[1024,3072]{1,0:T(8,128)}, bf16[1024,3072]{1,0:T(8,128)(2,1)}) fusion(bf16[1024,768]{1,0:T(8,128)(2,1)S(1)} %fusion.10.refs_2_, bf16[2,768,3072]{2,1,0:T(8,128)(2,1)S(1)} %copy-done.9), kind=kOutput, calls=%fused_computation.9 | convolution fusion | flops 4863295488 | bytes 25165824 | tf_op jit(solution)/shard_map/td,df->tf/dot_general | solution.py:42
  32.8 0.0 copy-done.12
  32.8 177.6 %grad_update.1 = (bf16[2,6,3072]{2,1,0:T(8,128)(2,1)}, bf16[2,24,768]{2,1,0:T(8,128)(2,1)}, f32[6,2,3072]{2,1,0:T(2,128)}, f32[2,24,768]{2,1,0:T(8,128)}, f32[6,...) custom-call(bf16[1024,768]{1,0:T(8,128)(2,1)} %refs_0_.1, ...), custom_call_target="tpu_custom_call" | custom-call | tf_op jit(solution)/shard_map/grad_update/pallas_call | solution.py:517
  210.4 0.0 copy-start.6
  210.4 0.9 copy-done.6
  211.3 0.0 copy-start.7
  211.3 0.9 copy-done.7
  212.2 58.0 %gather_weights.1 = (bf16[2,4,4,48,3072]{4,3,2,1,0:T(8,128)(2,1)S(1)}, bf16[2,4,4,4,48,768]{5,4,3,2,1,0:T(8,128)(2,1)S(1)}) custom-call(bf16[2,6,3072]{2,1,0:T(8,128)(2,1)S(1)} %copy-done.6, bf16[2,24,768]{2,1,0:T(8,128)(2,1)S(1)} %copy-done.7), custom_call_target="tpu_custom_call" | custom-call | tf_op jit(solution)/shard_map/gather_weights/pallas_call | solution.py:694
  270.2 0.0 copy-start
  270.2 0.9 copy-done
  271.1 0.0 copy-start.1
  271.1 0.9 copy-done.1
  272.0 0.0 copy-start.2
  272.0 0.9 copy-done.2
  272.9 0.0 copy-start.3
  272.9 0.9 copy-done.3
  273.8 0.0 copy-start.4
  273.8 0.9 copy-done.4
  274.7 0.0 copy-start.5
  274.7 0.9 copy-done.5
  275.6 0.0 copy-start.8
  275.7 0.7 copy-done.8
  276.3 7.0 %finish.1 = (bf16[2,4,4,48,3072]{4,3,2,1,0:T(8,128)(2,1)}, bf16[2,4,4,4,48,768]{5,4,3,2,1,0:T(8,128)(2,1)}, f32[6,2,3072]{2,1,0:T(2,128)}, f32[2,24,768]{2,1,0:T...) custom-call(bf16[2,4,4,48,3072]{4,3,2,1,0:T(8,128)(2,1)S(1)} %get-tu, ...), custom_call_target="tpu_custom_call" | custom-call | tf_op jit(solution)/shard_map/finish/pallas_call | solution.py:722
  283.4 0.5 slice.15
  (1 shorter events, 0.0 us)
Async XLA Ops:
  1.9 12.0 %copy-start.10 = (bf16[2,3072,768]{2,1,0:T(8,128)(2,1)S(1)}, bf16[2,3072,768]{2,1,0:T(8,128)(2,1)}, u32[]{:S(2)}) copy-start(bf16[2,3072,768]{2,1,0:T(8,128)(2,1)} %refs_8_.1) | copy-start | bytes 28311556
  13.9 5.1 %copy-start.11 = (bf16[1024,3072]{1,0:T(8,128)(2,1)}, bf16[1024,3072]{1,0:T(8,128)(2,1)S(1)}, u32[]{:S(2)}) copy-start(bf16[1024,3072]{1,0:T(8,128)(2,1)S(1)} %get-tuple-element.52.refs_3_) | copy-start | bytes 18874372
  13.9 6.0 %copy-start.9 = (bf16[2,768,3072]{2,1,0:T(8,128)(2,1)S(1)}, bf16[2,768,3072]{2,1,0:T(8,128)(2,1)}, u32[]{:S(2)}) copy-start(bf16[2,768,3072]{2,1,0:T(8,128)(2,1)} %refs_7_.1) | copy-start | bytes 28311556
  19.9 12.9 %copy-start.12 = (bf16[1024,768]{1,0:T(8,128)(2,1)}, bf16[1024,768]{1,0:T(8,128)(2,1)S(1)}, u32[]{:S(2)}) copy-start(bf16[1024,768]{1,0:T(8,128)(2,1)S(1)} %fusion.10.refs_2_) | copy-start | bytes 4718596
  210.4 0.9 copy-start.6
  211.3 0.9 copy-start.7
  270.2 0.9 copy-start
  271.1 0.9 copy-start.1
  272.0 0.9 copy-start.2
  272.9 0.9 copy-start.3
  273.8 0.9 copy-start.4
  274.7 0.9 copy-start.5
  275.6 0.7 copy-start.8

commit v2 on v1

--- a/solution.py
+++ b/solution.py
@@ -23,6 +23,9 @@
 LANES = 128
 PAIR = 2
 PHASES = 3
+FULL_VMEM = 67043328
+WEIGHT_LIMIT = 4194304
+AHEAD = 4
 SENDS = 6
 F32 = jnp.float32
 BF16 = jnp.bfloat16
@@ -83,23 +86,23 @@
         return self.half(phase, 0, 0, dict(x=0, y=0, z=0))[1]
 
 
-def make_units(up_cols, down_cols):
-    u, d = up_cols // PAIR, down_cols // 3
-    return [
-        Unit("down", 1, 0, PAIR * d, "xyz"),
-        Unit("down", 1, PAIR * d, d, "xzy"),
-        Unit("up", 1, 0, u, "zyx"),
-        Unit("up", 1, u, u, "yzx"),
-        Unit("up", 0, 0, u, "zyx"),
-        Unit("up", 0, u, u, "yzx"),
-        Unit("down", 0, 0, d, "xyz"),
-        Unit("down", 0, d, d, "yzx"),
-        Unit("down", 0, PAIR * d, d, "zxy"),
-    ]
+def column_groups(make, specs, up_cols, down_cols):
+    groups = []
+    for spec in specs:
+        k, first, count = map(int, spec[1:4])
+        kind, part = ("up", up_cols // PAIR) if spec[0] == "u" else ("down", down_cols // 3)
+        groups.append(make(kind, k, first * part, count * part, spec[4:]))
+    return groups
+
+
+REDUCE = ("d102xyz", "d121zyx", "u101zyx", "u111yzx")
+REDUCE_LATE = ("u001zyx", "u011yzx", "d001zyx", "d011xyz", "d021xyz")
+GATHER = ("d102zyx", "d002yzx", "d121xzy", "d021xyz")
+GATHER_LATE = ("u101yz", "u111zy", "u001yz", "u011zy")
 
 
 def serve_order(slots, ready, phases, tail, moved_per_us):
-    rate, hop = 43000.0, 3.0
+    rate, hop = 44000.0, 3.0
     link, now, plan = {}, 0.0, []
     ready, state, late = list(ready), [0] * len(ready), [0.0] * len(ready)
     ends = [PAIR * len(p) + tail for p in phases]
@@ -123,7 +126,7 @@
             served.append((i, state[i]))
             now = max(now, ready[i])
             if state[i]:
-                now += 0.3 + 8 * phases[i][(state[i] - 1) // PAIR if state[i] <= PAIR * len(phases[i]) else -1][1] / moved_per_us
+                now += 0.05 + 8 * phases[i][(state[i] - 1) // PAIR if state[i] <= PAIR * len(phases[i]) else -1][1] / moved_per_us
             if phase < len(phases[i]):
                 ready[i] = send(phases[i][phase])
                 if middle:
@@ -240,7 +243,7 @@
         return pltpu.make_async_copy(w_up.at[1, rows], w_wide, load_sem.at[2])
 
     def load_a(source, t):
-        return pltpu.make_async_copy(source.at[:, pl.ds(pl.multiple_of(t % 8 * wide, LANES), wide)], a_tile.at[t % PAIR], a_sem.at[t % PAIR])
+        return pltpu.make_async_copy(source.at[:, pl.ds(pl.multiple_of(t % 8 * wide, LANES), wide)], a_tile.at[t % AHEAD], a_sem.at[t % AHEAD])
 
     def tile_columns(t):
         half = jnp.where(t < n_tiles // PAIR, 1 - core, core)
@@ -258,7 +261,8 @@
             pl.when(stage == n)(pltpu.make_async_copy(source.at[:, cols], s_tile.at[slot], s_sem.at[slot]).start)
 
     load_right.start()
-    load_a(act_three, 0).start()
+    for t in range(AHEAD - 1):
+        load_a(act_three, t).start()
     load_outer.start()
     load_tile(0, False)
     load_wide(0).start()
@@ -346,82 +350,83 @@
         u = units[i]
         return remote(stage_down.at[z, :, :, :, u.off:u.off + u.cols], acc[i].at[z], down_send.at[i, z], down_recv.at[i, z], partner)
 
-    def down_grad(source, following, group, steps):
+    def down_grad(source, following, group, mine, steps):
+        columns = core if mine else 1 - core
+
         def tile(t, carry):
             for k, served in enumerate(steps):
                 serve_at((t, k), served)
+            z, y = t // PAIR, pl.ds(t % PAIR * 2, 2)
+            if mine:
+                pl.when(t % PAIR == 0)(lambda: [down_piece(i, z).wait_recv() for i in group] and None)
             load_a(source, t).wait()
-            pl.when(t < 15)(lambda: load_a(source, t + 1).start())
+            later = t + AHEAD - 1
+            pl.when(later < 8)(lambda: load_a(source, later).start())
             if following is not None:
-                pl.when(t == 15)(lambda: load_a(following, 0).start())
-            columns = jnp.where(t < 8, 1 - core, core)
-            value = dot(a_tile[t % PAIR], right[:, pl.ds(pl.multiple_of(columns * down_half, LANES), down_half)], (0, 0))
+                pl.when(later >= 8)(lambda: load_a(following, later).start())
+            value = dot(a_tile[t % AHEAD], right[:, pl.ds(pl.multiple_of(columns * down_half, LANES), down_half)], (0, 0))
             value = value.reshape(PAIR, RING, ROWS, down_half)
-            z, y = t % 8 // PAIR, pl.ds(t % PAIR * 2, 2)
-
-            @pl.when(t < 8)
-            def _():
+            if mine:
+                for i in group:
+                    acc[i][z, y] += value[..., units[i].off:units[i].off + units[i].cols]
+            else:
                 stage_down[z, y] = value
                 pl.when(t % PAIR == 1)(lambda: [down_piece(i, z).start() for i in group] and None)
-
-            @pl.when(t >= 8)
-            def _():
-                pl.when(t % PAIR == 0)(lambda: [down_piece(i, z).wait_recv() for i in group] and None)
-                for i in group:
-                    acc[i][z, y] += value[..., units[i].off:units[i].off + units[i].cols]
             return carry
 
-        lax.fori_loop(0, 16, tile, 0)
+        lax.fori_loop(0, 8, tile, 0)
 
     def up_piece(n):
         cols = pl.ds(pl.multiple_of(n % 3 * piece_cols, piece_cols), piece_cols)
         return remote(stage_up.at[:, :, :, cols], acc_up.at[n // 6, n // 3 % PAIR, :, :, :, cols], up_send.at[n], up_recv.at[n], partner)
 
-    def up_tile(at, carry):
-        for k, steps in enumerate(plan["up"]):
-            serve_at((at, k), steps)
-
-        @pl.when(at == n_tiles)
-        def _():
-            load_next.start()
-            for n in range(PHASES):
-                load_wide(n).wait()
-                right[:, n * piece_cols:(n + 1) * piece_cols] = dot(inner[...], w_wide[...], (1, 1)).astype(BF16)
-                if n < 2:
-                    load_wide(n + 1).start()
-            load_next.wait()
-
-        load_tile(at, True)
-        pl.when(at < PAIR * n_tiles - 1)(lambda: load_tile(at + 1, False))
-        stage, t = at // n_tiles, at % n_tiles
-        cols = tile_columns(t)
-        inner[:, cols] = (dot(right[...], w_tile[at % PAIR], (1, 1)) * s_tile[at % PAIR]).astype(BF16)
-        n = stage * 6 + t % 6
-        place = pl.ds(pl.multiple_of(t % 3 * piece_cols, piece_cols), piece_cols)
-        pl.when((t < 6) & (n > 2))(lambda: up_piece(n - 3).wait_send())
-        pl.when(t >= 6)(lambda: up_piece(n).wait_recv())
-        rows = outer.shape[1] // PAIR
-        for r in range(2):
-            value = dot(outer[:, r * rows:(r + 1) * rows], inner[:, cols], (0, 0)).reshape(PAIR, RING, ROWS, piece_cols)
-
-            @pl.when(t < 6)
-            def _():
-                stage_up[PAIR * r:PAIR * r + 2, :, :, place] = value
-
-            @pl.when(t >= 6)
-            def _():
-                acc_up[stage, t // 3 % PAIR, PAIR * r:PAIR * r + 2, :, :, place] += value
-        pl.when(t < 6)(lambda: up_piece(n).start())
-        return carry
+    def up_grad(stage, mine, steps):
+        start = stage * n_tiles + mine * 6
+
+        def tile(t, carry):
+            for k, served in enumerate(steps):
+                serve_at((t, k), served)
+            at = start + t
+            n = stage * 6 + t
+            if mine:
+                up_piece(n).wait_recv()
+            else:
+                pl.when(n > 2)(lambda: up_piece(n - 3).wait_send())
+            load_tile(at, True)
+            pl.when(at < PAIR * n_tiles - 1)(lambda: load_tile(at + 1, False))
+            cols = tile_columns(at % n_tiles)
+            inner[:, cols] = (dot(right[...], w_tile[at % PAIR], (1, 1)) * s_tile[at % PAIR]).astype(BF16)
+            place = pl.ds(pl.multiple_of(t % 3 * piece_cols, piece_cols), piece_cols)
+            value = dot(outer[...], inner[:, cols], (0, 0)).reshape(RING, RING, ROWS, piece_cols)
+            if mine:
+                acc_up[stage, t // 3, :, :, :, place] += value
+            else:
+                stage_up[:, :, :, place] = value
+                up_piece(n).start()
+            return carry
+
+        lax.fori_loop(0, 6, tile, 0)
 
     load_right.wait()
-    down_grad(act_three, act_one, (0, 1), ())
+    down_grad(act_three, act_three, (0, 1), False, ())
+    down_grad(act_three, act_one, (0, 1), True, ())
     load_outer.wait()
-    lax.fori_loop(0, PAIR * n_tiles, up_tile, 0)
+    up_grad(0, False, plan["up"][:6])
+    up_grad(0, True, plan["up"][6:12])
+    load_next.start()
+    for n in range(PHASES):
+        load_wide(n).wait()
+        right[:, n * piece_cols:(n + 1) * piece_cols] = dot(inner[...], w_wide[...], (1, 1)).astype(BF16)
+        if n < 2:
+            load_wide(n + 1).start()
+    load_next.wait()
+    up_grad(1, False, plan["up"][12:18])
+    up_grad(1, True, plan["up"][18:])
     for i in (0, 1):
         for z in range(RING):
             down_piece(i, z).wait_send()
-    down_grad(act_one, None, (6, 7, 8), plan["down"])
+    down_grad(act_one, act_one, (6, 7, 8), False, plan["down"][:8])
+    down_grad(act_one, None, (6, 7, 8), True, plan["down"][8:])
     for i, s in plan["end"]:
         serve(i, s)
 
@@ -487,12 +492,12 @@
 def grad_update(tensors, master, avg, sq, learn_rate, clip_norm):
     tokens, down_cols = tensors[0].shape
     up_cols = tensors[3].shape[1]
-    units = make_units(up_cols // PAIR, down_cols // PAIR)
+    units = column_groups(Unit, REDUCE + REDUCE_LATE, up_cols // PAIR, down_cols // PAIR)
     phases = [[(u.order[p], half_bytes(u.half_shape(p), F32)) for p in range(PHASES)] for u in units]
-    slots = [(12.0, (0, 1))]
-    slots += [(1.3 + (t == 11) * 7, {8: (2,), 11: (3,), 20: (4,), 23: (5,)}.get(t, ())) for t in range(24)]
-    slots += [(0.75, (6, 7, 8) if t == 15 else ()) for t in range(16)]
-    steps = serve_order(slots, [None] * len(units), phases, 1, 1500000.0)
+    slots = [(11.0, (0, 1))]
+    slots += [(1.7 + (t == 11) * 8, {8: (2,), 11: (3,), 20: (4,), 23: (5,)}.get(t, ())) for t in range(24)]
+    slots += [(0.6, (6, 7, 8) if t == 15 else ()) for t in range(16)]
+    steps = serve_order(slots, [None] * len(units), phases, 1, 12000000.0)
     plan = dict(up=steps[1:25], down=steps[25:41], end=steps[41])
     master, avg, sq = [(up.transpose(1, 0, 2), down) for up, down in (master, avg, sq)]
     blocks = [(PAIR, 6, up_cols), (PAIR, HALF, down_cols)]
@@ -507,11 +512,11 @@
     scratch += [pltpu.VMEM((RING, RING, RING, ROWS, down_cols // PAIR), F32), pltpu.VMEM((RING, RING, ROWS, 3 * piece), F32)]
     scratch += [pltpu.VMEM((tokens, up_cols), BF16), pltpu.VMEM((tokens, down_cols), BF16), pltpu.VMEM((tokens, down_cols), BF16)]
     scratch += [pltpu.VMEM((PAIR, piece, down_cols), BF16), pltpu.VMEM((PAIR, tokens, piece), F32)]
-    scratch += [pltpu.VMEM((PAIR, tokens, up_cols // 8), BF16), pltpu.VMEM((piece, up_cols), BF16)]
+    scratch += [pltpu.VMEM((AHEAD, tokens, up_cols // 8), BF16), pltpu.VMEM((piece, up_cols), BF16)]
     n = len(units)
     dma = pltpu.SemaphoreType.DMA
     scratch += [dma((n, RING)), dma((n, RING)), dma((12,)), dma((12,)), dma((n * PHASES * SENDS,)), dma((n * PHASES * SENDS,)), dma((n,)), dma((n,))]
-    scratch += [dma((PAIR, 7)), dma((PAIR, 8)), dma((PAIR, 15)), dma((PAIR, 16)), dma((2,)), dma((2,)), dma((2,)), dma((3,))]
+    scratch += [dma((PAIR, 16)), dma((PAIR, 16)), dma((PAIR, 16)), dma((PAIR, 16)), dma((PAIR,)), dma((PAIR,)), dma((AHEAD,)), dma((PHASES,))]
     vmem, smem, any_space = [pl.BlockSpec(memory_space=s) for s in (pltpu.VMEM, pltpu.SMEM, pl.ANY)]
     state = [jax.ShapeDtypeStruct(a.shape, F32) for a in master]
     return pl.pallas_call(
@@ -520,7 +525,7 @@
         in_specs=[any_space] * len(tensors) + [vmem] * 6 + [smem] * 2,
         out_specs=[vmem] * 9,
         scratch_shapes=scratch,
-        compiler_params=pltpu.CompilerParams(collective_id=0, has_side_effects=True, vmem_limit_bytes=67043328),
+        compiler_params=pltpu.CompilerParams(collective_id=0, has_side_effects=True, vmem_limit_bytes=FULL_VMEM),
         name="grad_update",
     )(*tensors, *master, *avg, *sq, learn_rate.reshape(1), clip_norm.reshape(1))
 
@@ -549,20 +554,6 @@
         if split:
             return tuple(index), tuple(shape) + (ROWS, self.cols)
         return tuple(index) + (pl.ds(HALF * h, HALF),), (HALF, self.cols)
-
-
-def make_gathers(up_cols, down_cols):
-    u, d = up_cols // PAIR, down_cols // 3
-    return [
-        Gather("down", 1, 0, PAIR * d, "zyx"),
-        Gather("down", 0, 0, PAIR * d, "yzx"),
-        Gather("down", 1, PAIR * d, d, "xzy"),
-        Gather("down", 0, PAIR * d, d, "xyz"),
-        Gather("up", 1, 0, u, "yz"),
-        Gather("up", 1, u, u, "zy"),
-        Gather("up", 0, 0, u, "yz"),
-        Gather("up", 0, u, u, "zy"),
-    ]
 
 
 def gather_kernel(units, events, up_ref, down_ref, out_up, out_down, *refs):
@@ -681,7 +672,7 @@
 
 def gather_weights(block_up, block_down):
     up_cols, down_cols = block_up.shape[2], block_down.shape[2]
-    units = make_gathers(up_cols // PAIR, down_cols // PAIR)
+    units = column_groups(Gather, GATHER + GATHER_LATE, up_cols // PAIR, down_cols // PAIR)
     here = dict(x=0, y=0, z=0)
     phases = [[(d, half_bytes(u.chunk(p, 0, here, 0)[1], BF16)) for p, d in enumerate(u.order)] for u in units]
     events = serve_order((), [2.0 if u.kind == "down" else 6.0 for u in units], phases, 0, math.inf)[0]
@@ -703,30 +694,36 @@
     return out_up, out_down
 
 
-def finish_kernel(*refs):
-    n = (len(refs) - 1) // PAIR
-    copies = []
-    for i in range(n):
-        src, dst = refs[i], refs[n + i]
-        for j in range(src.shape[0] * 2 if len(src.shape) > 3 else 1):
-            at = (j // PAIR, pl.ds(j % PAIR * 2, 2)) if len(src.shape) > 3 else slice(None)
-            copies.append(pltpu.make_async_copy(src.at[at], dst.at[at], refs[-1].at[i, j]))
+def finish_weights_kernel(up, down, out_up, out_down, sems):
+    copies = [pltpu.make_async_copy(src.at[k, z], dst.at[k, z], sems.at[i, k, z]) for i, (src, dst) in enumerate(((up, out_up), (down, out_down))) for k in range(PAIR) for z in range(RING)]
     for copy in copies:
         copy.start()
     for copy in copies:
         copy.wait()
 
 
-def finish(arrays):
+def finish_state_kernel(*refs):
+    n = len(refs) // 3
+    into = [pltpu.make_async_copy(src, buf, refs[-1].at[i]) for i, (src, buf) in enumerate(zip(refs[:n], refs[PAIR * n:-1]))]
+    back = [pltpu.make_async_copy(buf, dst, refs[-1].at[i]) for i, (buf, dst) in enumerate(zip(refs[PAIR * n:-1], refs[n:]))]
+    for copy in into:
+        copy.start()
+    for one, other in zip(into, back):
+        one.wait()
+        other.start()
+    for copy in back:
+        copy.wait()
+
+
+def finish(kernel, arrays, scratch, limit):
     any_space = pl.BlockSpec(memory_space=pl.ANY)
     return pl.pallas_call(
-        finish_kernel,
+        kernel,
         out_shape=[jax.ShapeDtypeStruct(a.shape, a.dtype) for a in arrays],
         in_specs=[any_space] * len(arrays),
         out_specs=[any_space] * len(arrays),
-        scratch_shapes=[pltpu.SemaphoreType.DMA((len(arrays), 4))],
-        compiler_params=pltpu.CompilerParams(vmem_limit_bytes=1024 * 1024),
-        name="finish",
+        scratch_shapes=scratch,
+        compiler_params=pltpu.CompilerParams(vmem_limit_bytes=limit),
     )(*arrays)
 
 
@@ -739,7 +736,10 @@
         act_one, slope_one, hidden, act_three, slope_three = forward(act_in, w_up, w_down)
         tensors = (act_in, grad_out, hidden, act_one, act_three, slope_one, slope_three, w_up, w_down)
         outs = grad_update(tensors, (master_up, master_down), (exp_avg_up, exp_avg_down), (exp_sq_up, exp_sq_down), learn_rate, clip_norm)
-        new_w_up, new_w_down, *state, norm = finish((*gather_weights(*outs[:2]), *outs[2:]))
+        dma = pltpu.SemaphoreType.DMA
+        small = [pltpu.VMEM(a.shape, F32) for a in outs[2:]]
+        *state, norm = finish(finish_state_kernel, outs[2:], small + [dma((len(small),))], FULL_VMEM)
+        new_w_up, new_w_down = finish(finish_weights_kernel, gather_weights(*outs[:2]), [dma((PAIR, PAIR, RING))], WEIGHT_LIMIT)
         state = [a.transpose(1, 0, 2) if i % PAIR == 0 else a for i, a in enumerate(state)]
         return (new_w_up.reshape(w_up.shape), new_w_down.reshape(w_down.shape), *state, norm[0, 0])
 

time: 286 us -> 255 us (0.89)
  Pallas kernels: 243 us -> 219 us
  local copies, waits for them, and re-layouts: 9.32 us -> 3.88 us
    pallas_call x1, Pallas kernels: 178 us -> 152 us  [grad_update(): pl.pallas_call(functools.partial(grad_update_kernel, units, plan), out_sh...]
    unnamed x26 -> x12, local copies, waits for them, and re-layouts: 8.81 us -> 2.68 us
    pallas_call x1 -> x2, Pallas kernels: 7.01 us -> 8.59 us  [finish(): pl.pallas_call(kernel, out_shape=[jax.ShapeDtypeStruct(a.shape, a.dtype)...]
where the time goes in v2:
time: 255 us
  Pallas kernels  219 us (86%)
  matrix products  29.9 us (12%)
  local copies, waits for them, and re-layouts  3.88 us (2%)
    pallas_call x1, Pallas kernels, grad_update(): pl.pallas_call(functools.partial(grad_update_kernel, units, plan), out_sh...  152 us
    pallas_call x1, Pallas kernels, gather_weights(): pl.pallas_call(functools.partial(gather_kernel, units, events), out_shape...  58.3 us
    dot_general x1, matrix products, forward(): jnp.einsum('td,df->tf', hidden, w_up[1], preferred_element_type=jnp.float32)  12.9 us
    dot_general x1, matrix products, forward(): jnp.einsum('td,df->tf', act_in, w_up[0], preferred_element_type=jnp.float32)  12 us
    pallas_call x2, Pallas kernels, finish(): pl.pallas_call(kernel, out_shape=[jax.ShapeDtypeStruct(a.shape, a.dtype)...  8.59 us

profile of v2, /device:TPU:1, one launch (start us, length us, event | category | flops | bytes accessed | tf_op | source)
XLA Modules:
  0.0 255.0 jit_solution(995332375758761808)
XLA Ops:
  1.9 0.0 copy-start.3
  1.9 12.0 %fusion.3 = (f32[1024,3072]{1,0:T(8,128)}, bf16[1024,3072]{1,0:T(8,128)(2,1)S(1)}) fusion(bf16[1024,768]{1,0:T(8,128)(2,1)} %refs_0_.1, bf16[2,768,3072]{2,1,0:T(8,128)(2,1)} %refs_7_.1), kind=kOutput, calls=%fused_computation.5 | convolution fusion | flops 4863295488 | bytes 25165824 | tf_op jit(solution)/shard_map/td,df->tf/dot_general | solution.py:41
  13.9 0.0 copy-start.4
  13.9 0.0 copy-done.3
  13.9 0.0 copy-start.2
  13.9 5.0 %fusion.10.refs_2_ = bf16[1024,768]{1,0:T(8,128)(2,1)S(1)} fusion(bf16[1024,3072]{1,0:T(8,128)(2,1)S(1)} %get-tuple-element.52.refs_3_, bf16[2,3072,768]{2,1,0:T(8,128)(2,1)S(1)} %copy-done.3), kind=kOutput, calls=%fused_computation.16 | convolution fusion | flops 4831838208 | bytes 12582912 | tf_op jit(solution)/shard_map/tf,fd->td/dot_general | solution.py:44
  19.0 0.0 copy-done.4
  19.0 0.9 copy-done.2
  19.9 0.0 copy-start.5
  19.9 12.9 %fusion.7 = (f32[1024,3072]{1,0:T(8,128)}, bf16[1024,3072]{1,0:T(8,128)(2,1)}) fusion(bf16[1024,768]{1,0:T(8,128)(2,1)S(1)} %fusion.10.refs_2_, bf16[2,768,3072]{2,1,0:T(8,128)(2,1)S(1)} %copy-done.2), kind=kOutput, calls=%fused_computation.9 | convolution fusion | flops 4863295488 | bytes 25165824 | tf_op jit(solution)/shard_map/td,df->tf/dot_general | solution.py:45
  32.8 0.0 copy-done.5
  32.8 152.1 %grad_update.1 = (bf16[2,6,3072]{2,1,0:T(8,128)(2,1)}, bf16[2,24,768]{2,1,0:T(8,128)(2,1)}, f32[6,2,3072]{2,1,0:T(2,128)}, f32[2,24,768]{2,1,0:T(8,128)}, f32[6,...) custom-call(bf16[1024,768]{1,0:T(8,128)(2,1)} %refs_0_.1, ...), custom_call_target="tpu_custom_call" | custom-call | tf_op jit(solution)/shard_map/grad_update/pallas_call | solution.py:522
  184.9 2.0 shard_map.188
  186.9 1.2 slice.15
  188.1 0.0 copy-start
  188.1 0.9 copy-done
  189.0 0.0 copy-start.1
  189.0 0.9 copy-done.1
  189.9 58.3 %gather_weights.1 = (bf16[2,4,4,48,3072]{4,3,2,1,0:T(8,128)(2,1)S(1)}, bf16[2,4,4,4,48,768]{5,4,3,2,1,0:T(8,128)(2,1)S(1)}) custom-call(bf16[2,6,3072]{2,1,0:T(8,128)(2,1)S(1)} %copy-done, bf16[2,24,768]{2,1,0:T(8,128)(2,1)S(1)} %copy-done.1), custom_call_target="tpu_custom_call" | custom-call | tf_op jit(solution)/shard_map/gather_weights/pallas_call | solution.py:685
  248.2 6.6 %shard_map.187 = (bf16[2,4,4,48,3072]{4,3,2,1,0:T(8,128)(2,1)}, bf16[2,4,4,4,48,768]{5,4,3,2,1,0:T(8,128)(2,1)}) custom-call(bf16[2,4,4,48,3072]{4,3,2,1,0:T(8,128)(2,1)S(1)} %get-tuple-element.31.up, bf16[2,4,4,4,48,768]{5,4,3,2,1,0:T(8,128)(2,1)S(1)} %get-tuple-element.32.down), custom_call_target="tpu_custom_call" | custom-call | tf_op jit(solution)/shard_map/pallas_call | solution.py:720
Async XLA Ops:
  1.9 12.0 %copy-start.3 = (bf16[2,3072,768]{2,1,0:T(8,128)(2,1)S(1)}, bf16[2,3072,768]{2,1,0:T(8,128)(2,1)}, u32[]{:S(2)}) copy-start(bf16[2,3072,768]{2,1,0:T(8,128)(2,1)} %refs_8_.1) | copy-start | bytes 28311556
  13.9 5.1 %copy-start.4 = (bf16[1024,3072]{1,0:T(8,128)(2,1)}, bf16[1024,3072]{1,0:T(8,128)(2,1)S(1)}, u32[]{:S(2)}) copy-start(bf16[1024,3072]{1,0:T(8,128)(2,1)S(1)} %get-tuple-element.52.refs_3_) | copy-start | bytes 18874372
  13.9 6.0 %copy-start.2 = (bf16[2,768,3072]{2,1,0:T(8,128)(2,1)S(1)}, bf16[2,768,3072]{2,1,0:T(8,128)(2,1)}, u32[]{:S(2)}) copy-start(bf16[2,768,3072]{2,1,0:T(8,128)(2,1)} %refs_7_.1) | copy-start | bytes 28311556
  19.9 12.9 %copy-start.5 = (bf16[1024,768]{1,0:T(8,128)(2,1)}, bf16[1024,768]{1,0:T(8,128)(2,1)S(1)}, u32[]{:S(2)}) copy-start(bf16[1024,768]{1,0:T(8,128)(2,1)S(1)} %fusion.10.refs_2_) | copy-start | bytes 4718596
  188.1 0.9 copy-start
  189.0 0.9 copy-start.1

commit v3 on v2

--- a/solution.py
+++ b/solution.py
@@ -95,8 +95,8 @@
     return groups
 
 
-REDUCE = ("d102xyz", "d121zyx", "u101zyx", "u111yzx")
-REDUCE_LATE = ("u001zyx", "u011yzx", "d001zyx", "d011xyz", "d021xyz")
+REDUCE = ("d102xzy", "d121xzy", "u101zyx", "u111yzx")
+REDUCE_LATE = ("u001zyx", "u011yzx", "d001xzy", "d011xzy", "d021xyz")
 GATHER = ("d102zyx", "d002yzx", "d121xzy", "d021xyz")
 GATHER_LATE = ("u101yz", "u111zy", "u001yz", "u011zy")
 
@@ -420,13 +420,13 @@
         if n < 2:
             load_wide(n + 1).start()
     load_next.wait()
-    up_grad(1, False, plan["up"][12:18])
-    up_grad(1, True, plan["up"][18:])
     for i in (0, 1):
         for z in range(RING):
             down_piece(i, z).wait_send()
     down_grad(act_one, act_one, (6, 7, 8), False, plan["down"][:8])
     down_grad(act_one, None, (6, 7, 8), True, plan["down"][8:])
+    up_grad(1, False, plan["up"][12:18])
+    up_grad(1, True, plan["up"][18:])
     for i, s in plan["end"]:
         serve(i, s)
 
@@ -494,11 +494,10 @@
     up_cols = tensors[3].shape[1]
     units = column_groups(Unit, REDUCE + REDUCE_LATE, up_cols // PAIR, down_cols // PAIR)
     phases = [[(u.order[p], half_bytes(u.half_shape(p), F32)) for p in range(PHASES)] for u in units]
-    slots = [(11.0, (0, 1))]
-    slots += [(1.7 + (t == 11) * 8, {8: (2,), 11: (3,), 20: (4,), 23: (5,)}.get(t, ())) for t in range(24)]
-    slots += [(0.6, (6, 7, 8) if t == 15 else ()) for t in range(16)]
+    slots = [(11.0, (0, 1))] + [(1.7 + (t == 11) * 8, {8: (2,), 11: (3,)}.get(t, ())) for t in range(12)]
+    slots += [(0.6, (6, 7, 8) if t == 15 else ()) for t in range(16)] + [(1.7, {8: (4,), 11: (5,)}.get(t, ())) for t in range(12)]
     steps = serve_order(slots, [None] * len(units), phases, 1, 12000000.0)
-    plan = dict(up=steps[1:25], down=steps[25:41], end=steps[41])
+    plan = dict(up=steps[1:13] + steps[29:41], down=steps[13:29], end=steps[41])
     master, avg, sq = [(up.transpose(1, 0, 2), down) for up, down in (master, avg, sq)]
     blocks = [(PAIR, 6, up_cols), (PAIR, HALF, down_cols)]
     piece = up_cols // 12

time: 255 us -> 251 us (0.984)
  Pallas kernels: 219 us -> 215 us
    pallas_call x1, Pallas kernels: 152 us -> 149 us  [grad_update(): pl.pallas_call(functools.partial(grad_update_kernel, units, plan), out_sh...]
where the time goes in v3:
time: 251 us
  Pallas kernels  215 us (86%)
  matrix products  29.9 us (12%)
  local copies, waits for them, and re-layouts  3.88 us (2%)
    pallas_call x1, Pallas kernels, grad_update(): pl.pallas_call(functools.partial(grad_update_kernel, units, plan), out_sh...  149 us
    pallas_call x1, Pallas kernels, gather_weights(): pl.pallas_call(functools.partial(gather_kernel, units, events), out_shape...  56.9 us
    dot_general x1, matrix products, forward(): jnp.einsum('td,df->tf', hidden, w_up[1], preferred_element_type=jnp.float32)  12.9 us
    dot_general x1, matrix products, forward(): jnp.einsum('td,df->tf', act_in, w_up[0], preferred_element_type=jnp.float32)  12 us
    pallas_call x2, Pallas kernels, finish(): pl.pallas_call(kernel, out_shape=[jax.ShapeDtypeStruct(a.shape, a.dtype)...  8.59 us
    dot_general x1, matrix products, forward(): jnp.einsum('tf,fd->td', act_one, w_down[0], preferred_element_type=jnp.fl...  5.04 us

profile of v3, /device:TPU:1, one launch (start us, length us, event | category | flops | bytes accessed | tf_op | source)
XLA Modules:
  0.0 250.8 jit_solution(16816993680238068968)
XLA Ops:
  1.9 0.0 copy-start.3
  1.9 12.0 %fusion.3 = (f32[1024,3072]{1,0:T(8,128)}, bf16[1024,3072]{1,0:T(8,128)(2,1)S(1)}) fusion(bf16[1024,768]{1,0:T(8,128)(2,1)} %refs_0_.1, bf16[2,768,3072]{2,1,0:T(8,128)(2,1)} %refs_7_.1), kind=kOutput, calls=%fused_computation.5 | convolution fusion | flops 4863295488 | bytes 25165824 | tf_op jit(solution)/shard_map/td,df->tf/dot_general | solution.py:41
  13.9 0.0 copy-start.4
  13.9 0.0 copy-done.3
  13.9 0.0 copy-start.2
  13.9 5.0 %fusion.10.refs_2_ = bf16[1024,768]{1,0:T(8,128)(2,1)S(1)} fusion(bf16[1024,3072]{1,0:T(8,128)(2,1)S(1)} %get-tuple-element.52.refs_3_, bf16[2,3072,768]{2,1,0:T(8,128)(2,1)S(1)} %copy-done.3), kind=kOutput, calls=%fused_computation.16 | convolution fusion | flops 4831838208 | bytes 12582912 | tf_op jit(solution)/shard_map/tf,fd->td/dot_general | solution.py:44
  19.0 0.0 copy-done.4
  19.0 0.9 copy-done.2
  19.9 0.0 copy-start.5
  19.9 12.9 %fusion.7 = (f32[1024,3072]{1,0:T(8,128)}, bf16[1024,3072]{1,0:T(8,128)(2,1)}) fusion(bf16[1024,768]{1,0:T(8,128)(2,1)S(1)} %fusion.10.refs_2_, bf16[2,768,3072]{2,1,0:T(8,128)(2,1)S(1)} %copy-done.2), kind=kOutput, calls=%fused_computation.9 | convolution fusion | flops 4863295488 | bytes 25165824 | tf_op jit(solution)/shard_map/td,df->tf/dot_general | solution.py:45
  32.8 0.0 copy-done.5
  32.8 149.4 %grad_update.1 = (bf16[2,6,3072]{2,1,0:T(8,128)(2,1)}, bf16[2,24,768]{2,1,0:T(8,128)(2,1)}, f32[6,2,3072]{2,1,0:T(2,128)}, f32[2,24,768]{2,1,0:T(8,128)}, f32[6,...) custom-call(bf16[1024,768]{1,0:T(8,128)(2,1)} %refs_0_.1, ...), custom_call_target="tpu_custom_call" | custom-call | tf_op jit(solution)/shard_map/grad_update/pallas_call | solution.py:521
  182.2 2.0 shard_map.188
  184.2 1.2 slice.15
  185.4 0.0 copy-start
  185.4 0.9 copy-done
  186.3 0.0 copy-start.1
  186.3 0.9 copy-done.1
  187.1 56.9 %gather_weights.1 = (bf16[2,4,4,48,3072]{4,3,2,1,0:T(8,128)(2,1)S(1)}, bf16[2,4,4,4,48,768]{5,4,3,2,1,0:T(8,128)(2,1)S(1)}) custom-call(bf16[2,6,3072]{2,1,0:T(8,128)(2,1)S(1)} %copy-done, bf16[2,24,768]{2,1,0:T(8,128)(2,1)S(1)} %copy-done.1), custom_call_target="tpu_custom_call" | custom-call | tf_op jit(solution)/shard_map/gather_weights/pallas_call | solution.py:684
  244.1 6.6 %shard_map.187 = (bf16[2,4,4,48,3072]{4,3,2,1,0:T(8,128)(2,1)}, bf16[2,4,4,4,48,768]{5,4,3,2,1,0:T(8,128)(2,1)}) custom-call(bf16[2,4,4,48,3072]{4,3,2,1,0:T(8,128)(2,1)S(1)} %get-tuple-element.31.up, bf16[2,4,4,4,48,768]{5,4,3,2,1,0:T(8,128)(2,1)S(1)} %get-tuple-element.32.down), custom_call_target="tpu_custom_call" | custom-call | tf_op jit(solution)/shard_map/pallas_call | solution.py:719
Async XLA Ops:
  1.9 12.0 %copy-start.3 = (bf16[2,3072,768]{2,1,0:T(8,128)(2,1)S(1)}, bf16[2,3072,768]{2,1,0:T(8,128)(2,1)}, u32[]{:S(2)}) copy-start(bf16[2,3072,768]{2,1,0:T(8,128)(2,1)} %refs_8_.1) | copy-start | bytes 28311556
  13.9 5.1 %copy-start.4 = (bf16[1024,3072]{1,0:T(8,128)(2,1)}, bf16[1024,3072]{1,0:T(8,128)(2,1)S(1)}, u32[]{:S(2)}) copy-start(bf16[1024,3072]{1,0:T(8,128)(2,1)S(1)} %get-tuple-element.52.refs_3_) | copy-start | bytes 18874372
  13.9 6.0 %copy-start.2 = (bf16[2,768,3072]{2,1,0:T(8,128)(2,1)S(1)}, bf16[2,768,3072]{2,1,0:T(8,128)(2,1)}, u32[]{:S(2)}) copy-start(bf16[2,768,3072]{2,1,0:T(8,128)(2,1)} %refs_7_.1) | copy-start | bytes 28311556
  19.9 12.9 %copy-start.5 = (bf16[1024,768]{1,0:T(8,128)(2,1)}, bf16[1024,768]{1,0:T(8,128)(2,1)S(1)}, u32[]{:S(2)}) copy-start(bf16[1024,768]{1,0:T(8,128)(2,1)S(1)} %fusion.10.refs_2_) | copy-start | bytes 4718596
  185.4 0.9 copy-start
  186.3 0.9 copy-start.1
